TPU v7x, 256 devices: a whole 4x4x8 slice. The times are simulated.
256 devices in a mesh: cls: 64 (over x, z, y_lo), dp: 4 (over y_hi, core).
Axes of the slice: x: 4, y: 4 (y_hi: 2, y_lo: 2; y = y_hi * 2 + y_lo), z: 8, core: 2. Of those that a mesh axis runs over, the one named last changes fastest.
Arguments:
- embeddings: bfloat16 [2048, 512], P(('dp', 'cls')), parts along dimension 0, may hold values from -4.4194174 to 4.4194174
- labels: int32 [2048], P(('dp', 'cls')), parts along dimension 0, may hold values from 0 to 262143
- centers: bfloat16 [1048576, 512], P(('dp', 'cls')), parts along dimension 0, may hold values from -3.0935922 to 3.0935922
Outputs:
- losses: float32 [2048], P(('dp', 'cls')), parts along dimension 0
- emb_grad: float32 [2048, 512], P(('dp', 'cls')), parts along dimension 0
- center_grad: float32 [1048576, 512], P(('dp', 'cls')), parts along dimension 0
There are 4 independent parts, one for each index of `dp`. A program takes and returns all parts, laid end to end along the dimension named above; each array names one. Nothing has to cross between parts.
All inputs are finite; a program needn't handle non-finite values.
Results may differ from a plain program's by a relative error of at most 0.0042.
Values may be sent and summed in bfloat16 or wider, within the bound.
A program may use at most 64 MiB of HBM per device.

v0:
```python
import math

import jax
import jax.numpy as jnp
from jax import lax
from jax.sharding import PartitionSpec as P

logit_scale = 64.0
margin_cosine = math.cos(0.5)
margin_sine = math.sin(0.5)
sine_soften = 0.04
norm_eps = 1e-06


def from_everyone(shard, axis):
    peers = lax.axis_size(axis)
    return lax.all_to_all(
        jnp.broadcast_to(shard[None], (peers, *shard.shape)), axis, 0, 0, tiled=True
    )


def in_order(blocks, dim):
    blocks = jnp.moveaxis(blocks, 0, dim)
    dims = blocks.shape
    return blocks.reshape(*dims[:dim], dims[dim] * dims[dim + 1], *dims[dim + 2 :])


def gathered_copies(shard, axis, dim):
    blocks = from_everyone(shard, axis)
    return in_order(blocks, dim)


def over_copies(shard, axis):
    return from_everyone(shard, axis).sum(axis=0)


def packed_total(arrays, axis):
    ends = [0]
    for a in arrays:
        ends.append(ends[-1] + a.size)
    subtotal = over_copies(jnp.concatenate([a.ravel() for a in arrays]), axis)
    return tuple((subtotal[b:e].reshape(a.shape) for a, b, e in zip(arrays, ends, ends[1:])))


def split_up(shard, dim, peers):
    dims = shard.shape
    blocks = shard.reshape(*dims[:dim], peers, dims[dim] // peers, *dims[dim + 1 :])
    return jnp.moveaxis(blocks, dim, 0)


def sum_at_owner(shard, axis, dim):
    blocks = split_up(shard, dim, lax.axis_size(axis))
    arrived = lax.all_to_all(blocks, axis, split_axis=0, concat_axis=0, tiled=True)
    return arrived.astype(jnp.float32).sum(axis=0)


def unit_rows(values):
    widened = values.astype(jnp.float32)
    inverse = lax.rsqrt(jnp.sum(widened * widened, axis=1, keepdims=True) + norm_eps)
    normed = widened * inverse
    return (inverse, normed, normed.astype(jnp.bfloat16))


def score_block(rows_hat, rows_label, center_block, class_base):
    cosine = jnp.dot(rows_hat, center_block.T, preferred_element_type=jnp.float32)
    local_col = rows_label - class_base
    is_owned = (local_col >= 0) & (local_col < center_block.shape[0])
    column = lax.broadcasted_iota(jnp.int32, cosine.shape, 1)
    target_mask = column == local_col[:, None]
    target_cos = jnp.sum(jnp.where(target_mask, cosine, 0.0), axis=1)
    target_sine = jnp.sqrt(1.0 + sine_soften - target_cos * target_cos)
    shifted = target_cos * margin_cosine - target_sine * margin_sine
    slopes = margin_cosine + margin_sine * target_cos / target_sine
    logits = jnp.where(target_mask, logit_scale * shifted[:, None], logit_scale * cosine)
    exp_terms = jnp.exp(logits - logit_scale)
    row_total = jnp.sum(exp_terms, axis=1)
    weighted = (logit_scale * exp_terms * jnp.where(target_mask, slopes[:, None], 1.0)).astype(
        jnp.bfloat16
    )
    target = jnp.where(is_owned, logit_scale * shifted, 0.0)
    columns = jnp.where(is_owned, local_col, -1).astype(jnp.int32)
    return (weighted, row_total, target, columns, jnp.where(is_owned, slopes, 0.0))


def row_term(weighted, center_block, totals, columns, slopes):
    product = jnp.dot(weighted, center_block, preferred_element_type=jnp.float32)
    picked = jnp.take(center_block, jnp.clip(columns, 0, center_block.shape[0] - 1), axis=0).astype(
        jnp.float32
    )
    return product / totals[:, None] - (logit_scale * slopes)[:, None] * picked


def class_term(weighted, scaled, rows_hat, columns, slopes, class_count):
    product = lax.dot_general(
        weighted, scaled, (((0,), (0,)), ((), ())), preferred_element_type=jnp.float32
    )
    drop_index = jnp.where(columns >= 0, columns, class_count)
    updates = -(logit_scale * slopes)[:, None] * rows_hat.astype(jnp.float32)
    return product.at[drop_index].add(updates, mode="drop")


def take_rows(whole, first_row, row_count):
    return lax.dynamic_slice_in_dim(whole, first_row, row_count, 0)


def per_device(embeddings, labels, centers):
    own_rows = embeddings.shape[0]
    class_count = centers.shape[0]
    class_base = lax.axis_index("cls") * class_count
    own_start = lax.axis_index("cls") * own_rows
    inv_x, units_x, emb_hat = unit_rows(embeddings)
    inv_w, units_w, center_hat = unit_rows(centers)
    rows_hat = gathered_copies(emb_hat, "cls", 0)
    rows_label = gathered_copies(labels, "cls", 0)
    weighted, row_total, target, columns, slopes = score_block(
        rows_hat, rows_label, center_hat, class_base
    )
    totals = row_total
    targets = target
    totals_all, targets_all = packed_total((totals, targets), "cls")
    own_total = take_rows(totals_all, own_start, own_rows)
    own_target = take_rows(targets_all, own_start, own_rows)
    losses = jnp.log(own_total) + logit_scale - own_target
    rows_hat = gathered_copies(emb_hat, "cls", 0)
    rows_label = gathered_copies(labels, "cls", 0)
    row_count = rows_hat.shape[0]
    weighted, row_total, target, columns, slopes = score_block(
        rows_hat, rows_label, center_hat, class_base
    )
    piece_totals = take_rows(totals_all, jnp.int32(0), row_count)
    scaled = (rows_hat.astype(jnp.float32) / piece_totals[:, None]).astype(jnp.bfloat16)
    grads_hat = class_term(weighted, scaled, rows_hat, columns, slopes, class_count)
    rows_out = row_term(weighted, center_hat, piece_totals, columns, slopes)
    grad_hat_w, rows_out = (grads_hat, rows_out)
    grad_hat_x = sum_at_owner(rows_out.astype(jnp.bfloat16), "cls", 0)
    emb_grad = inv_x * (grad_hat_x - units_x * jnp.sum(units_x * grad_hat_x, axis=1, keepdims=True))
    center_grad = inv_w * (
        grad_hat_w - units_w * jnp.sum(units_w * grad_hat_w, axis=1, keepdims=True)
    )
    return (losses, emb_grad, center_grad)


def solution(mesh):
    in_specs = (P(("dp", "cls"), None), P(("dp", "cls")), P(("dp", "cls"), None))
    out_specs = (P(("dp", "cls")), P(("dp", "cls"), None), P(("dp", "cls"), None))
    return jax.shard_map(
        per_device, mesh=mesh, in_specs=in_specs, out_specs=out_specs, check_vma=False
    )
```

profile of v0, /device:TPU:8, one launch (start us, length us, event | category | flops | bytes accessed | tf_op | source)
XLA Modules:
  0.0 122.5 jit_solution(4518268095324731753)
XLA Ops:
  0.6 1.3 %broadcast_in_dim.56 = s32[64,1,8]{2,1,0:T(1,128)} broadcast(s32[8]{0:T(128)} %param.4), dimensions={2} | broadcast | bytes 2080 | tf_op jit(solution)/shard_map/broadcast_in_dim | solution.py:18
  1.9 12.9 %all-to-all-start = ((s32[64,1,8]{2,1,0:T(1,128)}), s32[64,1,8]{2,1,0:T(1,128)S(1)}, u32[]{:S(2)}, u32[]{:S(2)}) async-start(s32[64,1,8]{2,1,0:T(1,128)} %broadcast_in_dim.56), calls=%async_computation | async-start | bytes 65536 | tf_op jit(solution)/shard_map/all_to_all | solution.py:17
  14.9 3.1 %fusion.6 = f32[4096]{0:T(1024)S(1)} fusion(bf16[4096,512]{1,0:T(8,128)(2,1)} %param.5), kind=kLoop, calls=%fused_computation.10 | loop fusion | flops 6287360 | bytes 4210688 | tf_op jit(solution)/shard_map/reduce_sum | solution.py:59
  18.0 0.8 fusion.27
  18.8 0.8 fusion.23
  19.6 4.6 %all-to-all-done = s32[64,1,8]{2,1,0:T(1,128)S(1)} async-done(((s32[64,1,8]{2,1,0:T(1,128)}), s32[64,1,8]{2,1,0:T(1,128)S(1)}, u32[]{:S(2)}, u32[]{:S(2)}) %all-to-all-start) | async-done | bytes 2080 | tf_op jit(solution)/shard_map/all_to_all | solution.py:17
  24.2 0.8 broadcast_in_dim.57
  25.0 6.6 %all-to-all-start.1 = ((bf16[64,8,512]{2,1,0:T(8,128)(2,1)}), bf16[64,8,512]{2,1,0:T(8,128)(2,1)S(1)}, u32[]{:S(2)}, u32[]{:S(2)}) async-start(bf16[64,8,512]{2,1,0:T(8,128)(2,1)} %broadcast_in_dim.57), calls=%async_computation.1 | async-start | bytes 1048576 | tf_op jit(solution)/shard_map/all_to_all | solution.py:17
  31.6 4.1 %fusion.2 = bf16[4096,512]{1,0:T(8,128)(2,1)} fusion(bf16[4096,512]{1,0:T(8,128)(2,1)} %param.5, f32[4096]{0:T(1024)S(1)} %add_rsqrt_fusion), kind=kLoop, calls=%fused_computation.6 | loop fusion | flops 6291456 | bytes 8404992 | tf_op jit(solution)/shard_map/convert_element_type | solution.py:61
  35.7 0.5 broadcast.341
  36.2 0.7 fusion.29
  37.0 0.1 sub.79
  37.0 0.1 sub.84
  37.1 10.4 %all-to-all-done.1 = bf16[64,8,512]{2,1,0:T(8,128)(2,1)S(1)} async-done(((bf16[64,8,512]{2,1,0:T(8,128)(2,1)}), bf16[64,8,512]{2,1,0:T(8,128)(2,1)S(1)}, u32[]{:S(2)}, u32[]{:S(2)}) %all-to-all-start.1) | async-done | bytes 524320 | tf_op jit(solution)/shard_map/all_to_all | solution.py:17
  47.6 4.7 %select_reduce_fusion = (f32[512]{0:T(512)S(1)}, f32[512,4096]{1,0:T(8,128)S(1)}) fusion(s32[512]{0:T(512)S(1)} %sub.79, bf16[4096,512]{1,0:T(8,128)(2,1)} %fusion.2, bf16[64,8,512]{2,1,0:T(8,128)(2,1)S(1)} %all-to-all-done.1), kind=kOutput, calls=%fused_computation.13 | convolution fusion | flops 2153774592 | bytes 13111296 | tf_op jit(solution)/shard_map/dot_general | solution.py:65
  52.2 5.5 %multiply_convert_fusion = (bf16[512,4096]{1,0:T(8,128)(2,1)}, f32[512]{0:T(512)S(1)}) fusion(f32[512,4096]{1,0:T(8,128)S(1)} %get-tuple-element.17, f32[512]{0:T(512)S(1)} %get-tuple-element.15, f32[512]{0:T(512)S(1)} %get-tuple-element.14, s32[512]{0:T(512)S(1)} %sub.79), kind=kLoop, calls=%fused_computation.11 | loop fusion | flops 18873856 | bytes 12591104 | tf_op jit(solution)/shard_map/convert_element_type | solution.py:77
  57.7 0.8 broadcast_in_dim.95
  58.5 7.2 %all-to-all-start.2 = ((f32[64,1,1024]{2,1,0:T(1,128)}), f32[64,1,1024]{2,1,0:T(1,128)S(1)}, u32[]{:S(2)}, u32[]{:S(2)}) async-start(f32[64,1,1024]{2,1,0:T(1,128)} %broadcast_in_dim.95), calls=%async_computation.2 | async-start | bytes 524288 | tf_op jit(solution)/shard_map/all_to_all | solution.py:17
  65.8 4.7 %gather_fusion = bf16[512,512]{1,0:T(8,128)(2,1)S(1)} fusion(bf16[4096,512]{1,0:T(8,128)(2,1)} %fusion.2, s32[1024]{0:T(1024)S(1)} %pad_clamp_fusion), kind=kCustom, calls=%fused_computation | custom fusion | bytes 1050624 | tf_op jit(solution)/shard_map/jit(_take)/gather | solution.py:87
  70.5 6.2 %all-to-all-done.2 = f32[64,1,1024]{2,1,0:T(1,128)S(1)} async-done(((f32[64,1,1024]{2,1,0:T(1,128)}), f32[64,1,1024]{2,1,0:T(1,128)S(1)}, u32[]{:S(2)}, u32[]{:S(2)}) %all-to-all-start.2) | async-done | bytes 262176 | tf_op jit(solution)/shard_map/all_to_all | solution.py:17
  76.7 0.2 reduce_sum.80
  76.9 6.6 %fusion.10 = bf16[64,8,512]{2,1,0:T(8,128)(2,1)} fusion(bf16[512,4096]{1,0:T(8,128)(2,1)} %get-tuple-element.7, bf16[4096,512]{1,0:T(8,128)(2,1)} %fusion.2, bf16[512,512]{1,0:T(8,128)(2,1)S(1)} %gather_fusion, f32[512]{0:T(512)S(1)} %get-tuple-element.4, f32[512]{0:T(512)S(1)} %get-tuple-element.10, pred[512]{0:T(512)(128)(4,1)S(1)} %compare_and_fusion), kind=kOutput, calls=%fused_computation.21 | convolution fusion | flops 2149056512 | bytes 9441792 | tf_op jit(solution)/shard_map/dot_general | solution.py:86
  83.5 6.5 %all-to-all-start.3 = ((bf16[64,8,512]{2,1,0:T(8,128)(2,1)}), bf16[64,8,512]{2,1,0:T(8,128)(2,1)S(1)}, u32[]{:S(2)}, u32[]{:S(2)}) async-start(bf16[64,8,512]{2,1,0:T(8,128)(2,1)} %fusion.10), calls=%async_computation.3 | async-start | bytes 1048576 | tf_op jit(solution)/shard_map/all_to_all | solution.py:53
  90.0 8.0 %fusion.13 = f32[4096,512]{1,0:T(8,128)} fusion(bf16[512,4096]{1,0:T(8,128)(2,1)} %get-tuple-element.7, bf16[64,8,512]{2,1,0:T(8,128)(2,1)S(1)} %all-to-all-done.1, f32[512]{0:T(512)S(1)} %get-tuple-element.10), kind=kOutput, calls=%fused_computation.25 | convolution fusion | flops 2148270080 | bytes 13109248 | tf_op jit(solution)/shard_map/dot_general | solution.py:94
  98.1 10.4 %scatter_custom_fusion = f32[4096,512]{1,0:T(8,128)} fusion(f32[4096,512]{1,0:T(8,128)} %fusion.13, s32[512]{0:T(512)S(1)} %bitcast.24, bf16[64,8,512]{2,1,0:T(8,128)(2,1)S(1)} %all-to-all-done.1, f32[512]{0:T(512)S(1)} %get-tuple-element.3), kind=kCustom, calls=%fused_computation.23 | custom fusion | flops 786432 | bytes 8914944 | tf_op jit(solution)/shard_map/scatter-add | solution.py:99
  108.5 0.0 copy-start
  108.5 0.0 copy-start.1
  108.5 6.3 %fusion.3 = f32[4096]{0:T(1024)S(1)} fusion(f32[4096,512]{1,0:T(8,128)} %scatter_custom_fusion, bf16[4096,512]{1,0:T(8,128)(2,1)} %param.5, f32[4096]{0:T(1024)S(1)} %add_rsqrt_fusion), kind=kLoop, calls=%fused_computation.7 | loop fusion | flops 8384512 | bytes 12615680 | tf_op jit(solution)/shard_map/reduce_sum | solution.py:138
  114.8 0.6 dynamic-slice_subtract_fusion
  115.4 0.0 copy-done
  115.4 1.4 %copy-done.1 = f32[4096,512]{1,0:T(8,128)S(1)} copy-done((f32[4096,512]{1,0:T(8,128)S(1)}, f32[4096,512]{1,0:T(8,128)}, u32[]{:S(2)}) %copy-start.1) | copy-done | bytes 8388632
  116.8 0.0 copy-start.2
  116.8 4.6 %fusion.5 = f32[4096,512]{1,0:T(8,128)} fusion(f32[4096,512]{1,0:T(8,128)S(1)} %copy-done.1, bf16[4096,512]{1,0:T(8,128)(2,1)S(1)} %copy-done, f32[4096]{0:T(1024)S(1)} %fusion.3, f32[4096]{0:T(1024)S(1)} %add_rsqrt_fusion), kind=kLoop, calls=%fused_computation.9 | loop fusion | flops 10485760 | bytes 21004288 | tf_op jit(solution)/shard_map/mul | solution.py:137
  121.5 0.0 all-to-all-done.3
  121.5 0.1 convert_reduce_fusion
  121.6 0.0 copy-done.2
  121.6 0.2 fusion.24
  121.8 0.7 fusion.26
  (8 shorter events, 0.1 us)
Async XLA Ops:
  1.9 22.3 %all-to-all-start = ((s32[64,1,8]{2,1,0:T(1,128)}), s32[64,1,8]{2,1,0:T(1,128)S(1)}, u32[]{:S(2)}, u32[]{:S(2)}) async-start(s32[64,1,8]{2,1,0:T(1,128)} %broadcast_in_dim.56), calls=%async_computation | async-start | bytes 65536 | tf_op jit(solution)/shard_map/all_to_all | solution.py:17
  25.0 22.5 %all-to-all-start.1 = ((bf16[64,8,512]{2,1,0:T(8,128)(2,1)}), bf16[64,8,512]{2,1,0:T(8,128)(2,1)S(1)}, u32[]{:S(2)}, u32[]{:S(2)}) async-start(bf16[64,8,512]{2,1,0:T(8,128)(2,1)} %broadcast_in_dim.57), calls=%async_computation.1 | async-start | bytes 1048576 | tf_op jit(solution)/shard_map/all_to_all | solution.py:17
  58.5 18.2 %all-to-all-start.2 = ((f32[64,1,1024]{2,1,0:T(1,128)}), f32[64,1,1024]{2,1,0:T(1,128)S(1)}, u32[]{:S(2)}, u32[]{:S(2)}) async-start(f32[64,1,1024]{2,1,0:T(1,128)} %broadcast_in_dim.95), calls=%async_computation.2 | async-start | bytes 524288 | tf_op jit(solution)/shard_map/all_to_all | solution.py:17
  83.5 38.0 %all-to-all-start.3 = ((bf16[64,8,512]{2,1,0:T(8,128)(2,1)}), bf16[64,8,512]{2,1,0:T(8,128)(2,1)S(1)}, u32[]{:S(2)}, u32[]{:S(2)}) async-start(bf16[64,8,512]{2,1,0:T(8,128)(2,1)} %fusion.10), calls=%async_computation.3 | async-start | bytes 1048576 | tf_op jit(solution)/shard_map/all_to_all | solution.py:53
  108.5 6.9 %copy-start = (bf16[4096,512]{1,0:T(8,128)(2,1)S(1)}, bf16[4096,512]{1,0:T(8,128)(2,1)}, u32[]{:S(2)}) copy-start(bf16[4096,512]{1,0:T(8,128)(2,1)} %param.5) | copy-start | bytes 12582916
  108.5 8.3 %copy-start.1 = (f32[4096,512]{1,0:T(8,128)S(1)}, f32[4096,512]{1,0:T(8,128)}, u32[]{:S(2)}) copy-start(f32[4096,512]{1,0:T(8,128)} %scatter_custom_fusion) | copy-start | bytes 25165828
  116.8 4.8 %copy-start.2 = (bf16[8,512]{1,0:T(8,128)(2,1)S(1)}, bf16[8,512]{1,0:T(8,128)(2,1)}, u32[]{:S(2)}) copy-start(bf16[8,512]{1,0:T(8,128)(2,1)} %param.3) | copy-start | bytes 24580
where the time goes:
time: 123 us; the launch traced here: 122 us
  other arithmetic  38.1 us (31%)
  starting transfers between devices  33.3 us (27%)
  waiting for transfers between devices  21.3 us (17%)
  matrix products  19.3 us (16%)
  local copies, waits for them, and re-layouts  9.77 us (8%)
    all_to_all x3, starting transfers between devices, from_everyone(): lax.all_to_all(jnp.broadcast_to(shard[None], (peers, *shard.shape)), axis...  26.7 us
    all_to_all x3, waiting for transfers between devices, from_everyone(): lax.all_to_all(jnp.broadcast_to(shard[None], (peers, *shard.shape)), axis...  21.3 us
    scatter-add x1, other arithmetic, class_term(): return product.at[drop_index].add(updates, mode='drop')  10.4 us
    dot_general x1, matrix products, class_term(): lax.dot_general(weighted, scaled, (((0,), (0,)), ((), ())), preferred_ele...  8.04 us
    dot_general x1, matrix products, row_term(): jnp.dot(weighted, center_block, preferred_element_type=jnp.float32)  6.59 us
    all_to_all x1, starting transfers between devices, sum_at_owner(): lax.all_to_all(blocks, axis, split_axis=0, concat_axis=0, tiled=True)  6.53 us
    reduce_sum x1, other arithmetic, per_device(): jnp.sum(units_w * grad_hat_w, axis=1, keepdims=True)  6.28 us
    convert_element_type x1, other arithmetic, score_block(): (logit_scale * exp_terms * jnp.where(target_mask, slopes[:, None], 1.0))....  5.47 us
  transfers between devices with their start and end apart: 4, of which 3 were waited for; matrix products, arithmetic and copies ran while one was open for 37% of the time, Pallas kernels for 0%

commit v1 on v0

v1 whole, which is shorter than its diff:
```python
import functools
import math

import jax
import jax.numpy as jnp
from jax import lax
from jax.experimental import pallas as pl
from jax.experimental.pallas import tpu as pltpu
from jax.sharding import PartitionSpec as P

MC = math.cos(0.5)
MS = math.sin(0.5)
EPS = 1e-06
NX, NY, NZ = 4, 2, 8
ROWS = 8
D = 512
C = 4096
B = 512
CB = 512
NCB = C // CB
F32 = jnp.float32
BF16 = jnp.bfloat16
ZOFF = (0, 1, 7, 2, 6, 3, 5, 4)


def pid(x, y, z):
    return x * (NY * NZ) + z * NY + y


def head_kernel(
    lab_ref, emb_ref, cen_ref,
    wt_ref, raw_ref, scaled_ref, coef_ref, lcol_ref, grad_ref, loss_ref,
    xg, lg, hat, hat_t, ehat, acc_n, acc_p, csend, crecv_y, crecv_x, crecv_z, ctot,
    dsend, drecv_x, drow, ysend, drecv_y, zown, zsend, drecv_z,
    cen_sem, send_sem, recv_sem,
):
    me = lax.axis_index("cls")
    x = me // (NY * NZ)
    z = (me % (NY * NZ)) // NY
    y = me % NY
    py = 1 - y
    ypeer = pid(x, py, z)
    xs = [(x + k) % NX for k in range(1, NX)]
    xpeers = [pid(v, y, z) for v in xs]
    zs = [(z + k) % NZ for k in ZOFF[1:]]
    zpeers = [pid(x, y, v) for v in zs]
    base = me * C

    def cen_copy(i):
        rows = pl.ds(i * CB, CB)
        return pltpu.make_async_copy(cen_ref.at[rows], raw_ref.at[rows], cen_sem.at[i])

    for i in range(NCB):
        cen_copy(i).start()

    barrier = pltpu.get_barrier_semaphore()
    for p in [ypeer] + xpeers + zpeers:
        pl.semaphore_signal(barrier, inc=1, device_id={"cls": p})

    lane = lax.broadcasted_iota(jnp.int32, (1, 128), 1)
    off = (y * NZ + z) * ROWS
    lrow = jnp.zeros((1, 128), jnp.int32)
    for r in range(ROWS):
        lrow = jnp.where(lane == off + r, lab_ref[r], lrow)
    lg[x, y, z] = lrow
    xg[x, y, z] = emb_ref[...]

    pl.semaphore_wait(barrier, 11)

    pending = []
    nsem = [0]

    def copy(src, dst, peer):
        i = nsem[0]
        nsem[0] += 1
        return pltpu.make_async_remote_copy(
            src_ref=src, dst_ref=dst, send_sem=send_sem.at[i], recv_sem=recv_sem.at[i],
            device_id={"cls": peer},
        )

    def go(src, dst, peer):
        c = copy(src, dst, peer)
        c.start()
        pending.append(c)
        return c

    ye = go(emb_ref, xg.at[x, y, z], ypeer)
    yl = go(lg.at[x, y, z], lg.at[x, y, z], ypeer)

    def norm_block(i):
        cen_copy(i).wait()
        rows = pl.ds(i * CB, CB)
        v = raw_ref[rows].astype(F32)
        inv = lax.rsqrt(jnp.sum(v * v, axis=1, keepdims=True) + EPS)
        hat[rows] = (v * inv).astype(BF16)

    def turn_block(i):
        rows = pl.ds(i * CB, CB)
        a = lax.broadcasted_iota(jnp.int32, (D, D), 0)
        b = lax.broadcasted_iota(jnp.int32, (D, D), 1)
        eye = jnp.where(a == b, 1.0, 0.0).astype(BF16)
        t = lax.dot_general(eye, hat[rows], (((1,), (1,)), ((), ())), preferred_element_type=F32)
        hat_t[i] = t.astype(BF16)

    norm_block(0)
    ye.wait_recv()
    yl.wait_recv()
    ze = [go(xg.at[x, :, z], xg.at[x, :, z], p) for p in zpeers]
    zl = [go(lg.at[x, :, z], lg.at[x, :, z], p) for p in zpeers]
    xe = []

    def forward(j):
        zj = (z + NZ - ZOFF[j]) % NZ
        for p in xpeers:
            xe.append(go(xg.at[x, :, zj], xg.at[x, :, zj], p))

    forward(0)
    for j in range(1, NZ):
        norm_block(j)
        ze[j - 1].wait_recv()
        forward(j)
    for c in zl:
        c.wait_recv()
    xl = [go(lg.at[x], lg.at[x], p) for p in xpeers]

    for i in range(NCB):
        turn_block(i)

    for c in xe + xl:
        c.wait_recv()

    labs = []
    for v in range(NX):
        e = xg[v].astype(F32)
        inv = lax.rsqrt(jnp.sum(e * e, axis=-1, keepdims=True) + EPS)
        ehat[pl.ds(v * 128, 128)] = (e * inv).reshape(128, D).astype(BF16)
        labs.append(jnp.sum(lg[v].reshape(NY * NZ, 128), axis=0, keepdims=True))
    lab = jnp.concatenate(labs, axis=1)
    lcol = lab - base
    owned = (lcol >= 0) & (lcol < C)
    lcol_ref[...] = jnp.broadcast_to(lcol, (8, B))

    def block(i, carry):
        t_acc, c_acc = carry
        rows = pl.ds(pl.multiple_of(i * CB, CB), CB)
        cos = lax.dot_general(
            hat[rows], ehat[...], (((1,), (1,)), ((), ())), preferred_element_type=F32
        )
        rid = lax.broadcasted_iota(jnp.int32, (CB, B), 0) + i * CB
        mask = rid == lcol
        c_acc += jnp.sum(jnp.where(mask, cos, 0.0).reshape(CB // 8, 8, B), axis=0)
        e = jnp.where(mask, 0.0, jnp.exp(64.0 * cos - 64.0))
        t_acc += jnp.sum(e.reshape(CB // 8, 8, B), axis=0)
        wt_ref[rows] = e.astype(BF16)
        return t_acc, c_acc

    zero = jnp.zeros((8, B), F32)
    t_acc, c_acc = lax.fori_loop(0, NCB, block, (zero, zero))
    t_part = jnp.sum(t_acc, axis=0, keepdims=True)
    tcos = jnp.sum(c_acc, axis=0, keepdims=True)
    tsin = jnp.sqrt(1.04 - tcos * tcos)
    shifted = tcos * MC - tsin * MS
    slope = jnp.where(owned, MC + MS * tcos / tsin, 0.0)
    et = jnp.where(owned, jnp.exp(64.0 * shifted - 64.0), 0.0)
    target = jnp.where(owned, 64.0 * shifted, 0.0)
    t_part = t_part + et
    for k in range(4):
        cols = slice(k * 128, (k + 1) * 128)
        csend[0, k : k + 1] = t_part[:, cols]
        csend[0, k + 4 : k + 5] = target[:, cols]
    cy = go(csend.at[0], crecv_y, ypeer)

    def n_block(i):
        rows = pl.ds(i * CB, CB)
        t = jnp.dot(hat_t[i], wt_ref[rows], preferred_element_type=F32)
        if i == 0:
            acc_n[...] = t
        else:
            acc_n[...] += t

    def p_block(i):
        rid = lax.broadcasted_iota(jnp.int32, (CB, B), 0) + i * CB
        hot = jnp.where(rid == lcol, 1.0, 0.0).astype(BF16)
        t = jnp.dot(hat_t[i], hot, preferred_element_type=F32)
        if i == 0:
            acc_p[...] = t
        else:
            acc_p[...] += t

    for i in range(4):
        n_block(i)
    cy.wait_recv()
    csend[1] = csend[0] + crecv_y[...]
    cx = [go(csend.at[1], crecv_x.at[k], p) for k, p in enumerate(xpeers)]
    for i in range(4, 8):
        n_block(i)
    p_block(0)
    for c in cx:
        c.wait_recv()
    csend[2] = csend[1] + crecv_x[0] + crecv_x[1] + crecv_x[2]
    cz = [go(csend.at[2], crecv_z.at[k], p) for k, p in enumerate(zpeers)]
    for i in range(1, 8):
        p_block(i)
    for c in cz:
        c.wait_recv()
    tot = csend[2]
    for k in range(7):
        tot = tot + crecv_z[k]
    ctot[...] = tot

    total = jnp.concatenate([ctot[k : k + 1] for k in range(4)], axis=1)
    inv_t = 1.0 / total
    coef_ref[...] = jnp.broadcast_to(slope * (et - total), (8, B))
    ca = 64.0 * inv_t
    cb = 64.0 * slope * (et * inv_t - 1.0)
    for k in range(4):
        cols = slice(k * 128, (k + 1) * 128)
        g = acc_n[:, cols] * ca[:, cols] + acc_p[:, cols] * cb[:, cols]
        acc_n[:, cols] = g
        dsend[k] = g.astype(BF16)
    dx = [go(dsend.at[v], drecv_x.at[k], p) for k, (v, p) in enumerate(zip(xs, xpeers))]

    for k in range(4):
        cols = slice(k * 128, (k + 1) * 128)
        col = jnp.broadcast_to(ca[:, cols], (128, 128)).T
        for j in range(4):
            dcols = slice(j * 128, (j + 1) * 128)
            v = ehat[pl.ds(k * 128, 128), dcols].astype(F32) * col
            scaled_ref[pl.ds(k * 128, 128), dcols] = v.astype(BF16)

    trow = ctot[pl.ds(x, 1)]
    grow = ctot[pl.ds(x + 4, 1)]
    lossv = jnp.log(trow) + 64.0 - grow
    lossv = jnp.broadcast_to(lossv, (8, 128))
    loss_ref[...] = pltpu.roll(lossv, (128 - off) % 128, 1)

    for c in dx:
        c.wait_recv()
    own = acc_n[:, pl.ds(pl.multiple_of(x * 128, 128), 128)]
    own = own + drecv_x[0].astype(F32) + drecv_x[1].astype(F32) + drecv_x[2].astype(F32)
    drow[...] = own.T.reshape(NY, 64, D)
    ysend[...] = drow[py].astype(BF16)
    dy = go(ysend, drecv_y, ypeer)
    dy.wait_recv()
    s = drow[y] + drecv_y[...].astype(F32)
    zown[...] = s.reshape(NZ, ROWS, D)
    zsend[...] = s.reshape(NZ, ROWS, D).astype(BF16)
    dz = [go(zsend.at[v], drecv_z.at[k], p) for k, (v, p) in enumerate(zip(zs, zpeers))]
    for c in dz:
        c.wait_recv()
    g = zown[z]
    for k in range(7):
        g = g + drecv_z[k].astype(F32)
    e = emb_ref[...].astype(F32)
    inv = lax.rsqrt(jnp.sum(e * e, axis=1, keepdims=True) + EPS)
    u = e * inv
    grad_ref[...] = inv * (g - u * jnp.sum(u * g, axis=1, keepdims=True))
    for c in pending:
        c.wait_send()


def class_kernel(
    lab_ref, wt_ref, raw_ref, scaled_ref, coef_ref, grad_ref, loss_ref,
    out_ref, gout_ref, lout_ref, buf, sem,
):
    gout_ref[...] = grad_ref[...]
    lout_ref[...] = loss_ref[...]
    copies = [None] * NCB
    for i in range(NCB):
        rows = slice(i * CB, (i + 1) * CB)
        w = wt_ref[rows]
        rid = lax.broadcasted_iota(jnp.int32, (CB, B), 0) + i * CB
        w = jnp.where(rid == lab_ref[0:1], coef_ref[0:1], w.astype(F32)).astype(BF16)
        g = jnp.dot(w, scaled_ref[...], preferred_element_type=F32)
        v = raw_ref[rows].astype(F32)
        inv = lax.rsqrt(jnp.sum(v * v, axis=1, keepdims=True) + EPS)
        dot = jnp.sum(v * g, axis=1, keepdims=True)
        if i >= 3:
            copies[i - 3].wait()
        buf[i % 3] = inv * g - (inv * inv * inv * dot) * v
        copies[i] = pltpu.make_async_copy(buf.at[i % 3], out_ref.at[rows], sem.at[i % 3])
        copies[i].start()
    for c in copies[-3:]:
        c.wait()


def per_device(embeddings, labels, centers):
    vm = pl.BlockSpec(memory_space=pltpu.VMEM)
    return pl.pallas_call(
        head_kernel,
        out_shape=(
            pltpu.VMEM((C, B), BF16),
            pltpu.VMEM((C, D), BF16),
            pltpu.VMEM((B, D), BF16),
            pltpu.VMEM((8, B), F32),
            pltpu.VMEM((8, B), jnp.int32),
            pltpu.VMEM((ROWS, D), F32),
            pltpu.VMEM((8, 128), F32),
        ),
        in_specs=[
            pl.BlockSpec(memory_space=pltpu.SMEM),
            vm,
            pl.BlockSpec(memory_space=pl.ANY),
        ],
        out_specs=(vm,) * 7,
        scratch_shapes=[
            pltpu.VMEM((NX, NY, NZ, ROWS, D), BF16),
            pltpu.VMEM((NX, NY, NZ, 1, 128), jnp.int32),
            pltpu.VMEM((C, D), BF16),
            pltpu.VMEM((NCB, D, CB), BF16),
            pltpu.VMEM((B, D), BF16),
            pltpu.VMEM((D, B), F32),
            pltpu.VMEM((D, B), F32),
            pltpu.VMEM((3, 8, 128), F32),
            pltpu.VMEM((8, 128), F32),
            pltpu.VMEM((3, 8, 128), F32),
            pltpu.VMEM((7, 8, 128), F32),
            pltpu.VMEM((8, 128), F32),
            pltpu.VMEM((NX, D, 128), BF16),
            pltpu.VMEM((3, D, 128), BF16),
            pltpu.VMEM((NY, 64, D), F32),
            pltpu.VMEM((64, D), BF16),
            pltpu.VMEM((64, D), BF16),
            pltpu.VMEM((NZ, ROWS, D), F32),
            pltpu.VMEM((NZ, ROWS, D), BF16),
            pltpu.VMEM((7, ROWS, D), BF16),
            pltpu.SemaphoreType.DMA((NCB,)),
            pltpu.SemaphoreType.DMA((70,)),
            pltpu.SemaphoreType.DMA((70,)),
        ],
        compiler_params=pltpu.CompilerParams(
            collective_id=0, has_side_effects=True, vmem_limit_bytes=40 * 1024 * 1024
        ),
        name="head",
    )(labels, embeddings, centers)


def whole(embeddings, labels, centers):
    wt, raw, scaled, coef, lcol, grad, loss = per_device(embeddings, labels, centers)
    vm = pl.BlockSpec(memory_space=pltpu.VMEM)
    out, grad, loss = pl.pallas_call(
        class_kernel,
        out_shape=(
            jax.ShapeDtypeStruct((C, D), F32),
            jax.ShapeDtypeStruct((ROWS, D), F32),
            jax.ShapeDtypeStruct((8, 128), F32),
        ),
        in_specs=[vm] * 7,
        out_specs=(pl.BlockSpec(memory_space=pl.ANY), vm, vm),
        scratch_shapes=[
            pltpu.VMEM((3, CB, D), F32),
            pltpu.SemaphoreType.DMA((3,)),
        ],
        compiler_params=pltpu.CompilerParams(vmem_limit_bytes=24 * 1024 * 1024),
        name="classes",
    )(lcol, wt, raw, scaled, coef, grad, loss)
    return loss[0, :ROWS], grad, out


def solution(mesh):
    in_specs = (P(("dp", "cls"), None), P(("dp", "cls")), P(("dp", "cls"), None))
    out_specs = (P(("dp", "cls")), P(("dp", "cls"), None), P(("dp", "cls"), None))
    return jax.shard_map(
        whole, mesh=mesh, in_specs=in_specs, out_specs=out_specs, check_vma=False
    )
```

time: 123 us -> 66.1 us (0.54)
  Pallas kernels: 0 us -> 60.4 us
  other arithmetic: 38.1 us -> 0 us
  starting transfers between devices: 33.3 us -> 0 us
  waiting for transfers between devices: 21.3 us -> 0 us
  matrix products: 19.3 us -> 0 us
  local copies, waits for them, and re-layouts: 9.77 us -> 4.05 us
    pallas_call x0 -> x2, Pallas kernels: none -> 60.4 us  [the longest x1 53.4 us: per_device(): pl.pallas_call(head_kernel, out_shape=(pltpu.VMEM((C, B), BF16), pltpu.VM...]
    all_to_all x4 -> x0, starting transfers between devices: 33.3 us -> none  [the longest x3 26.7 us: from_everyone(): lax.all_to_all(jnp.broadcast_to(shard[None], (peers, *shard.shape)), axis...]
    all_to_all x4 -> x0, waiting for transfers between devices: 21.3 us -> none  [the longest x3 21.3 us: from_everyone(): lax.all_to_all(jnp.broadcast_to(shard[None], (peers, *shard.shape)), axis...]
    dot_general x3 -> x0, matrix products: 19.3 us -> none  [the longest x1 8.04 us: class_term(): lax.dot_general(weighted, scaled, (((0,), (0,)), ((), ())), preferred_ele...]
    reduce_sum x6 -> x0, other arithmetic: 10.7 us -> none  [the longest x1 6.28 us: per_device(): jnp.sum(units_w * grad_hat_w, axis=1, keepdims=True)]
    scatter-add x1 -> x0, other arithmetic: 10.4 us -> none  [class_term(): return product.at[drop_index].add(updates, mode='drop')]
    convert_element_type x3 -> x0, other arithmetic: 10.3 us -> none  [the longest x1 5.47 us: score_block(): (logit_scale * exp_terms * jnp.where(target_mask, slopes[:, None], 1.0))....]
    mul x2 -> x0, other arithmetic: 5.33 us -> none  [the longest x1 4.64 us: per_device(): inv_w * (grad_hat_w - units_w * jnp.sum(units_w * grad_hat_w, axis=1, kee...]
  transfers between devices with their start and end apart: 4 -> 0, of which waited for: 3 -> 0; matrix products, arithmetic and copies ran while one was open for 37% -> 0% of each run, Pallas kernels for 0% -> 0%
where the time goes in v1:
time: 66.1 us; the launch traced here: 65.1 us
  Pallas kernels  60.4 us (91%)
  local copies, waits for them, and re-layouts  4.05 us (6%)
    pallas_call x1, Pallas kernels, per_device(): pl.pallas_call(head_kernel, out_shape=(pltpu.VMEM((C, B), BF16), pltpu.VM...  53.4 us
    pallas_call x1, Pallas kernels, whole(): pl.pallas_call(class_kernel, out_shape=(jax.ShapeDtypeStruct((C, D), F32)...  7.01 us
    unnamed x6, local copies, waits for them, and re-layouts  3.53 us

profile of v1, /device:TPU:8, one launch (start us, length us, event | category | flops | bytes accessed | tf_op | source)
XLA Modules:
  0.0 65.1 jit_solution(4676499445544533083)
XLA Ops:
  0.6 0.0 copy-start
  0.6 2.2 %copy-done = bf16[4096,512]{1,0:T(8,128)(2,1)S(1)} copy-done((bf16[4096,512]{1,0:T(8,128)(2,1)S(1)}, bf16[4096,512]{1,0:T(8,128)(2,1)}, u32[]{:S(2)}) %copy-start) | copy-done | bytes 4194328
  2.8 0.0 copy-start.1
  2.8 0.7 %copy-done.1 = bf16[8,512]{1,0:T(8,128)(2,1)S(1)} copy-done((bf16[8,512]{1,0:T(8,128)(2,1)S(1)}, bf16[8,512]{1,0:T(8,128)(2,1)}, u32[]{:S(2)}) %copy-start.1) | copy-done | bytes 8216
  3.5 0.0 copy-start.2
  3.5 0.7 %copy-done.2 = s32[8]{0:T(128)S(1)} copy-done((s32[8]{0:T(128)S(1)}, s32[8]{0:T(128)}, u32[]{:S(2)}) %copy-start.2) | copy-done | bytes 56
  4.2 53.4 %head.1 = (bf16[4096,512]{1,0:T(8,128)(2,1)S(1)}, bf16[4096,512]{1,0:T(8,128)(2,1)S(1)}, bf16[512,512]{1,0:T(8,128)(2,1)S(1)}, f32[8,512]{1,0:T(8,128)S(1)}, s32...) custom-call(s32[8]{0:T(128)S(1)} %copy-done.2, bf16[8,512]{1,0:T(8,128)(2,1)S(1)} %copy-done.1, ...), custom_call_target="tpu_custom_call" | custom-call | tf_op jit(solution)/shard_map/head/pallas_call | solution.py:289
  57.5 7.0 %classes.1 = (f32[4096,512]{1,0:T(8,128)}, f32[8,512]{1,0:T(8,128)}, f32[8,128]{1,0:T(8,128)S(1)}) custom-call(s32[8,512]{1,0:T(8,128)S(1)} %get-tuple-element.13.lab_ref, bf16[4096,512]{1,0:T(8,128)(2,1)S(1)} %get-tuple-element.14.wt_ref, bf16[4096,512]{1,0:T(8,128)(2,1)S(1)} %get-tuple-element.15.raw_ref, ...), custom_call_target="tpu_custom_call" | custom-call | tf_op jit(solution)/shard_map/classes/pallas_call | solution.py:341
  64.6 0.5 slice_bitcast_fusion
Async XLA Ops:
  0.6 2.2 %copy-start = (bf16[4096,512]{1,0:T(8,128)(2,1)S(1)}, bf16[4096,512]{1,0:T(8,128)(2,1)}, u32[]{:S(2)}) copy-start(bf16[4096,512]{1,0:T(8,128)(2,1)} %cen_ref.1) | copy-start | bytes 12582916
  2.8 0.7 %copy-start.1 = (bf16[8,512]{1,0:T(8,128)(2,1)S(1)}, bf16[8,512]{1,0:T(8,128)(2,1)}, u32[]{:S(2)}) copy-start(bf16[8,512]{1,0:T(8,128)(2,1)} %emb_ref.1) | copy-start | bytes 24580
  3.5 0.7 %copy-start.2 = (s32[8]{0:T(128)S(1)}, s32[8]{0:T(128)}, u32[]{:S(2)}) copy-start(s32[8]{0:T(128)} %lab_ref.1) | copy-start | bytes 100

commit v2 on v1

--- a/solution.py
+++ b/solution.py
@@ -28,9 +28,9 @@
 
 
 def head_kernel(
-    lab_ref, emb_ref, cen_ref,
-    wt_ref, raw_ref, scaled_ref, coef_ref, lcol_ref, grad_ref, loss_ref,
-    xg, lg, hat, hat_t, ehat, acc_n, acc_p, csend, crecv_y, crecv_x, crecv_z, ctot,
+    lab_hbm, emb_hbm, cen_ref,
+    out_ref, grad_ref, loss_ref,
+    lab_ref, emb_ref, wt_ref, raw_ref, scaled_ref, coef_ref, xg, lg, hat, hat_t, ehat, acc_n, acc_p, csend, crecv_y, crecv_x, crecv_z, ctot,
     dsend, drecv_x, drow, ysend, drecv_y, zown, zsend, drecv_z,
     cen_sem, send_sem, recv_sem,
 ):
@@ -42,6 +42,7 @@
     ypeer = pid(x, py, z)
     xs = [(x + k) % NX for k in range(1, NX)]
     xpeers = [pid(v, y, z) for v in xs]
+    ypeers = [pid(x, py, (z + k) % NZ) for k in ZOFF]
     zs = [(z + k) % NZ for k in ZOFF[1:]]
     zpeers = [pid(x, y, v) for v in zs]
     base = me * C
@@ -50,22 +51,47 @@
         rows = pl.ds(i * CB, CB)
         return pltpu.make_async_copy(cen_ref.at[rows], raw_ref.at[rows], cen_sem.at[i])
 
+    small = [
+        pltpu.make_async_copy(lab_hbm, lab_ref, cen_sem.at[NCB]),
+        pltpu.make_async_copy(emb_hbm, emb_ref, cen_sem.at[NCB + 1]),
+    ]
+    for c in small:
+        c.start()
     for i in range(NCB):
         cen_copy(i).start()
 
     barrier = pltpu.get_barrier_semaphore()
-    for p in [ypeer] + xpeers + zpeers:
+    for p in ypeers + xpeers + zpeers:
         pl.semaphore_signal(barrier, inc=1, device_id={"cls": p})
 
     lane = lax.broadcasted_iota(jnp.int32, (1, 128), 1)
     off = (y * NZ + z) * ROWS
     lrow = jnp.zeros((1, 128), jnp.int32)
+    for c in small:
+        c.wait()
     for r in range(ROWS):
         lrow = jnp.where(lane == off + r, lab_ref[r], lrow)
     lg[x, y, z] = lrow
     xg[x, y, z] = emb_ref[...]
 
-    pl.semaphore_wait(barrier, 11)
+    def norm_block(i):
+        cen_copy(i).wait()
+        rows = pl.ds(i * CB, CB)
+        v = raw_ref[rows].astype(F32)
+        inv = lax.rsqrt(jnp.sum(v * v, axis=1, keepdims=True) + EPS)
+        hat[rows] = (v * inv).astype(BF16)
+
+    def turn_block(i):
+        rows = pl.ds(i * CB, CB)
+        a = lax.broadcasted_iota(jnp.int32, (D, D), 0)
+        b = lax.broadcasted_iota(jnp.int32, (D, D), 1)
+        eye = jnp.where(a == b, 1.0, 0.0).astype(BF16)
+        t = lax.dot_general(eye, hat[rows], (((1,), (1,)), ((), ())), preferred_element_type=F32)
+        hat_t[i] = t.astype(BF16)
+
+    for i in range(NCB):
+        norm_block(i)
+    pl.semaphore_wait(barrier, 18)
 
     pending = []
     nsem = [0]
@@ -84,47 +110,32 @@
         pending.append(c)
         return c
 
-    ye = go(emb_ref, xg.at[x, y, z], ypeer)
-    yl = go(lg.at[x, y, z], lg.at[x, y, z], ypeer)
-
-    def norm_block(i):
-        cen_copy(i).wait()
-        rows = pl.ds(i * CB, CB)
-        v = raw_ref[rows].astype(F32)
-        inv = lax.rsqrt(jnp.sum(v * v, axis=1, keepdims=True) + EPS)
-        hat[rows] = (v * inv).astype(BF16)
-
-    def turn_block(i):
-        rows = pl.ds(i * CB, CB)
-        a = lax.broadcasted_iota(jnp.int32, (D, D), 0)
-        b = lax.broadcasted_iota(jnp.int32, (D, D), 1)
-        eye = jnp.where(a == b, 1.0, 0.0).astype(BF16)
-        t = lax.dot_general(eye, hat[rows], (((1,), (1,)), ((), ())), preferred_element_type=F32)
-        hat_t[i] = t.astype(BF16)
-
-    norm_block(0)
-    ye.wait_recv()
-    yl.wait_recv()
-    ze = [go(xg.at[x, :, z], xg.at[x, :, z], p) for p in zpeers]
-    zl = [go(lg.at[x, :, z], lg.at[x, :, z], p) for p in zpeers]
+    own_e, own_l = emb_ref, lg.at[x, y, z]
+    arr = []
+    for k, off_z in enumerate(ZOFF):
+        yz = []
+        if k:
+            yz.append((y, zpeers[k - 1]))
+        yz.append((py, ypeers[k]))
+        for src_y, p in yz:
+            ce = go(own_e, xg.at[x, y, z], p)
+            cl = go(own_l, lg.at[x, y, z], p)
+            arr.append((ce, cl, src_y, (z + NZ - off_z) % NZ))
     xe = []
 
-    def forward(j):
-        zj = (z + NZ - ZOFF[j]) % NZ
+    def forward(v, w):
         for p in xpeers:
-            xe.append(go(xg.at[x, :, zj], xg.at[x, :, zj], p))
-
-    forward(0)
-    for j in range(1, NZ):
-        norm_block(j)
-        ze[j - 1].wait_recv()
-        forward(j)
-    for c in zl:
-        c.wait_recv()
+            xe.append(go(xg.at[x, v, w], xg.at[x, v, w], p))
+
+    forward(y, z)
+    for j, (ce, cl, v, w) in enumerate(arr):
+        if j % 2 == 0:
+            turn_block(j // 2)
+        ce.wait_recv()
+        forward(v, w)
+    for ce, cl, v, w in arr:
+        cl.wait_recv()
     xl = [go(lg.at[x], lg.at[x], p) for p in xpeers]
-
-    for i in range(NCB):
-        turn_block(i)
 
     for c in xe + xl:
         c.wait_recv()
@@ -138,7 +149,6 @@
     lab = jnp.concatenate(labs, axis=1)
     lcol = lab - base
     owned = (lcol >= 0) & (lcol < C)
-    lcol_ref[...] = jnp.broadcast_to(lcol, (8, B))
 
     def block(i, carry):
         t_acc, c_acc = carry
@@ -234,6 +244,18 @@
     lossv = jnp.broadcast_to(lossv, (8, 128))
     loss_ref[...] = pltpu.roll(lossv, (128 - off) % 128, 1)
 
+    def class_block(i):
+        rows = pl.ds(i * CB, CB)
+        rid = lax.broadcasted_iota(jnp.int32, (CB, B), 0) + i * CB
+        w = jnp.where(rid == lcol, coef_ref[0:1], wt_ref[rows].astype(F32)).astype(BF16)
+        g = jnp.dot(w, scaled_ref[...], preferred_element_type=F32)
+        v = raw_ref[rows].astype(F32)
+        inv = lax.rsqrt(jnp.sum(v * v, axis=1, keepdims=True) + EPS)
+        dot = jnp.sum(v * g, axis=1, keepdims=True)
+        out_ref[rows] = inv * g - (inv * inv * inv * dot) * v
+
+    for i in range(4):
+        class_block(i)
     for c in dx:
         c.wait_recv()
     own = acc_n[:, pl.ds(pl.multiple_of(x * 128, 128), 128)]
@@ -241,11 +263,15 @@
     drow[...] = own.T.reshape(NY, 64, D)
     ysend[...] = drow[py].astype(BF16)
     dy = go(ysend, drecv_y, ypeer)
+    for i in range(4, 6):
+        class_block(i)
     dy.wait_recv()
     s = drow[y] + drecv_y[...].astype(F32)
     zown[...] = s.reshape(NZ, ROWS, D)
     zsend[...] = s.reshape(NZ, ROWS, D).astype(BF16)
     dz = [go(zsend.at[v], drecv_z.at[k], p) for k, (v, p) in enumerate(zip(zs, zpeers))]
+    for i in range(6, 8):
+        class_block(i)
     for c in dz:
         c.wait_recv()
     g = zown[z]
@@ -259,51 +285,38 @@
         c.wait_send()
 
 
-def class_kernel(
-    lab_ref, wt_ref, raw_ref, scaled_ref, coef_ref, grad_ref, loss_ref,
-    out_ref, gout_ref, lout_ref, buf, sem,
-):
+def write_kernel(val_ref, grad_ref, loss_ref, out_ref, gout_ref, lout_ref, sem):
+    copies = []
+    for i in range(NCB):
+        rows = pl.ds(i * CB, CB)
+        c = pltpu.make_async_copy(val_ref.at[rows], out_ref.at[rows], sem.at[i])
+        c.start()
+        copies.append(c)
     gout_ref[...] = grad_ref[...]
-    lout_ref[...] = loss_ref[...]
-    copies = [None] * NCB
-    for i in range(NCB):
-        rows = slice(i * CB, (i + 1) * CB)
-        w = wt_ref[rows]
-        rid = lax.broadcasted_iota(jnp.int32, (CB, B), 0) + i * CB
-        w = jnp.where(rid == lab_ref[0:1], coef_ref[0:1], w.astype(F32)).astype(BF16)
-        g = jnp.dot(w, scaled_ref[...], preferred_element_type=F32)
-        v = raw_ref[rows].astype(F32)
-        inv = lax.rsqrt(jnp.sum(v * v, axis=1, keepdims=True) + EPS)
-        dot = jnp.sum(v * g, axis=1, keepdims=True)
-        if i >= 3:
-            copies[i - 3].wait()
-        buf[i % 3] = inv * g - (inv * inv * inv * dot) * v
-        copies[i] = pltpu.make_async_copy(buf.at[i % 3], out_ref.at[rows], sem.at[i % 3])
-        copies[i].start()
-    for c in copies[-3:]:
+    lout_ref[...] = loss_ref[0:1, 0:ROWS]
+    for c in copies:
         c.wait()
 
 
-def per_device(embeddings, labels, centers):
+def whole(embeddings, labels, centers):
     vm = pl.BlockSpec(memory_space=pltpu.VMEM)
-    return pl.pallas_call(
+    hbm = pl.BlockSpec(memory_space=pltpu.HBM)
+    val, grad, loss = pl.pallas_call(
         head_kernel,
         out_shape=(
+            pltpu.VMEM((C, D), F32),
+            pltpu.VMEM((ROWS, D), F32),
+            pltpu.VMEM((8, 128), F32),
+        ),
+        in_specs=[hbm] * 3,
+        out_specs=(vm,) * 3,
+        scratch_shapes=[
+            pltpu.SMEM((ROWS,), jnp.int32),
+            pltpu.VMEM((ROWS, D), BF16),
             pltpu.VMEM((C, B), BF16),
             pltpu.VMEM((C, D), BF16),
             pltpu.VMEM((B, D), BF16),
             pltpu.VMEM((8, B), F32),
-            pltpu.VMEM((8, B), jnp.int32),
-            pltpu.VMEM((ROWS, D), F32),
-            pltpu.VMEM((8, 128), F32),
-        ),
-        in_specs=[
-            pl.BlockSpec(memory_space=pltpu.SMEM),
-            vm,
-            pl.BlockSpec(memory_space=pl.ANY),
-        ],
-        out_specs=(vm,) * 7,
-        scratch_shapes=[
             pltpu.VMEM((NX, NY, NZ, ROWS, D), BF16),
             pltpu.VMEM((NX, NY, NZ, 1, 128), jnp.int32),
             pltpu.VMEM((C, D), BF16),
@@ -324,37 +337,29 @@
             pltpu.VMEM((NZ, ROWS, D), F32),
             pltpu.VMEM((NZ, ROWS, D), BF16),
             pltpu.VMEM((7, ROWS, D), BF16),
-            pltpu.SemaphoreType.DMA((NCB,)),
-            pltpu.SemaphoreType.DMA((70,)),
-            pltpu.SemaphoreType.DMA((70,)),
+            pltpu.SemaphoreType.DMA((NCB + 2,)),
+            pltpu.SemaphoreType.DMA((110,)),
+            pltpu.SemaphoreType.DMA((110,)),
         ],
         compiler_params=pltpu.CompilerParams(
-            collective_id=0, has_side_effects=True, vmem_limit_bytes=40 * 1024 * 1024
+            collective_id=0, has_side_effects=True, vmem_limit_bytes=50 * 1024 * 1024
         ),
         name="head",
     )(labels, embeddings, centers)
-
-
-def whole(embeddings, labels, centers):
-    wt, raw, scaled, coef, lcol, grad, loss = per_device(embeddings, labels, centers)
-    vm = pl.BlockSpec(memory_space=pltpu.VMEM)
     out, grad, loss = pl.pallas_call(
-        class_kernel,
+        write_kernel,
         out_shape=(
             jax.ShapeDtypeStruct((C, D), F32),
             jax.ShapeDtypeStruct((ROWS, D), F32),
-            jax.ShapeDtypeStruct((8, 128), F32),
+            jax.ShapeDtypeStruct((1, ROWS), F32),
         ),
-        in_specs=[vm] * 7,
-        out_specs=(pl.BlockSpec(memory_space=pl.ANY), vm, vm),
-        scratch_shapes=[
-            pltpu.VMEM((3, CB, D), F32),
-            pltpu.SemaphoreType.DMA((3,)),
-        ],
-        compiler_params=pltpu.CompilerParams(vmem_limit_bytes=24 * 1024 * 1024),
-        name="classes",
-    )(lcol, wt, raw, scaled, coef, grad, loss)
-    return loss[0, :ROWS], grad, out
+        in_specs=[vm] * 3,
+        out_specs=(pl.BlockSpec(memory_space=pltpu.HBM), vm, vm),
+        scratch_shapes=[pltpu.SemaphoreType.DMA((NCB,))],
+        compiler_params=pltpu.CompilerParams(vmem_limit_bytes=4 * 1024 * 1024),
+        name="write",
+    )(val, grad, loss)
+    return loss.reshape(ROWS), grad, out
 
 
 def solution(mesh):

time: 66.1 us -> 58.1 us (0.88); the launches traced: 65.1 us -> 58 us
  local copies, waits for them, and re-layouts: 4.05 us -> 0 us
  Pallas kernels: 60.4 us -> 57.2 us
    unnamed x6 -> x0, local copies, waits for them, and re-layouts: 3.53 us -> none
    pallas_call x2, Pallas kernels: 60.4 us -> 57.2 us  [the longest x1 53.2 us: whole(): pl.pallas_call(head_kernel, out_shape=(pltpu.VMEM((C, D), F32), pltpu.VME...]
where the time goes in v2:
time: 58.1 us; the launch traced here: 58 us
  Pallas kernels  57.2 us (98%)
  between operations  0.8 us (1%)
    pallas_call x1, Pallas kernels, whole(): pl.pallas_call(head_kernel, out_shape=(pltpu.VMEM((C, D), F32), pltpu.VME...  53.2 us
    pallas_call x1, Pallas kernels, whole(): pl.pallas_call(write_kernel, out_shape=(jax.ShapeDtypeStruct((C, D), F32)...  3.98 us

profile of v2, /device:TPU:8, one launch (start us, length us, event | category | flops | bytes accessed | tf_op | source)
XLA Modules:
  0.0 58.0 jit_solution(3073201676696034600)
XLA Ops:
  0.6 53.2 %head.1 = (f32[4096,512]{1,0:T(8,128)S(1)}, f32[8,512]{1,0:T(8,128)S(1)}, f32[8,128]{1,0:T(8,128)S(1)}) custom-call(s32[8]{0:T(128)} %lab_hbm.1, bf16[8,512]{1,0:T(8,128)(2,1)} %emb_hbm.1, bf16[4096,512]{1,0:T(8,128)(2,1)} %cen_ref.1), custom_call_target="tpu_custom_call" | custom-call | tf_op jit(solution)/shard_map/head/pallas_call | solution.py:304
  53.8 4.0 %write.1 = (f32[4096,512]{1,0:T(8,128)}, f32[8,512]{1,0:T(8,128)}, f32[1,8]{1,0:T(1,128)}) custom-call(f32[4096,512]{1,0:T(8,128)S(1)} %get-tuple-element.9.val_ref, f32[8,512]{1,0:T(8,128)S(1)} %get-tuple-element.10.grad_ref, f32[8,128]{1,0:T(8,128)S(1)} %get-tuple-element.11.loss_ref), custom_call_target="tpu_custom_call" | custom-call | tf_op jit(solution)/shard_map/write/pallas_call | solution.py:349

commit v3 on v2

v3 whole, which is shorter than its diff:
```python
import functools
import math

import jax
import jax.numpy as jnp
from jax import lax
from jax.experimental import pallas as pl
from jax.experimental.pallas import tpu as pltpu
from jax.sharding import PartitionSpec as P

MC = math.cos(0.5)
MS = math.sin(0.5)
EPS = 1e-06
NX, NY, NZ = 4, 2, 8
ROWS = 8
D = 512
C = 4096
B = 512
CB = 512
NCB = C // CB
F32 = jnp.float32
BF16 = jnp.bfloat16
ZOFF = (0, 1, 7, 2, 6, 3, 5, 4)
KQ = (0, 1, 3, 2)
HB = B // 2
NK = 6
LOG2E = 64.0 / math.log(2.0)


def pid(x, y, z):
    return x * (NY * NZ) + z * NY + y


def class_rows(i, lcol_ref, coef_ref, wt_ref, raw_ref, scaled_ref):
    rows = slice(i * CB, (i + 1) * CB)
    rid = lax.broadcasted_iota(jnp.int32, (CB, B), 0) + i * CB
    w = jnp.where(rid == lcol_ref[0:1], coef_ref[0:1], wt_ref[rows].astype(F32)).astype(BF16)
    g = jnp.dot(w, scaled_ref[...], preferred_element_type=F32)
    v = raw_ref[rows].astype(F32)
    inv = lax.rsqrt(jnp.sum(v * v, axis=1, keepdims=True) + EPS)
    dot = jnp.sum(v * g, axis=1, keepdims=True)
    return inv * g - (inv * inv * inv * dot) * v


def head_kernel(
    lab_hbm, emb_hbm, cen_ref,
    out_ref, grad_ref, loss_ref, wt_ref, raw_ref, scaled_ref, coef_ref, lcol_ref,
    lab_ref, emb_ref, xg, lg, hat, hat_t, ehat, cosb,
    own_n, pt, csend, crecv_x, crecv_yz, ctot,
    psend, precv_x, prow, precv, dsend, drecv_x, drow, drow_b, drecv,
    cen_sem, send_sem, recv_sem,
):
    me = lax.axis_index("cls")
    x = me // (NY * NZ)
    z = (me % (NY * NZ)) // NY
    y = me % NY
    py = 1 - y
    planes = [(x + NX - k) % NX for k in KQ]
    xpeers = [pid(v, y, z) for v in planes[1:]]
    yz_ids = []
    for k in ZOFF:
        if k:
            yz_ids.append((y, k))
        yz_ids.append((py, k))
    yzpeers = [pid(x, v, (z + k) % NZ) for v, k in yz_ids]
    base = me * C

    def cen_copy(i):
        rows = pl.ds(i * CB, CB)
        return pltpu.make_async_copy(cen_ref.at[rows], raw_ref.at[rows], cen_sem.at[i])

    small = [
        pltpu.make_async_copy(lab_hbm, lab_ref, cen_sem.at[NCB]),
        pltpu.make_async_copy(emb_hbm, emb_ref, cen_sem.at[NCB + 1]),
    ]
    for c in small:
        c.start()
    for i in range(NCB):
        cen_copy(i).start()

    barrier = pltpu.get_barrier_semaphore()
    for p in yzpeers + xpeers:
        pl.semaphore_signal(barrier, inc=1, device_id={"cls": p})

    lane = lax.broadcasted_iota(jnp.int32, (1, 128), 1)
    off = (y * NZ + z) * ROWS
    lrow = jnp.zeros((1, 128), jnp.int32)
    for c in small:
        c.wait()
    for r in range(ROWS):
        lrow = jnp.where(lane == off + r, lab_ref[r], lrow)
    lg[y, z, x] = lrow
    xg[x, y, z] = emb_ref[...]

    def norm_block(i):
        cen_copy(i).wait()
        rows = pl.ds(i * CB, CB)
        v = raw_ref[rows].astype(F32)
        inv = lax.rsqrt(jnp.sum(v * v, axis=1, keepdims=True) + EPS)
        hat[rows] = (v * inv).astype(BF16)

    def turn_block(i):
        rows = pl.ds(i * CB, CB)
        a = lax.broadcasted_iota(jnp.int32, (D, D), 0)
        b = lax.broadcasted_iota(jnp.int32, (D, D), 1)
        eye = jnp.where(a == b, 1.0, 0.0).astype(BF16)
        t = lax.dot_general(eye, hat[rows], (((1,), (1,)), ((), ())), preferred_element_type=F32)
        hat_t[:, rows] = t.astype(BF16)

    for i in range(NCB):
        norm_block(i)
    pl.semaphore_wait(barrier, 18)

    pending = []
    nsem = [0]

    def go(src, dst, peer):
        i = nsem[0]
        nsem[0] += 1
        c = pltpu.make_async_remote_copy(
            src_ref=src, dst_ref=dst, send_sem=send_sem.at[i], recv_sem=recv_sem.at[i],
            device_id={"cls": peer},
        )
        c.start()
        pending.append(c)
        return c

    lsl = lg.at[y, z, x]
    xl = [go(lsl, lsl, p) for p in xpeers]
    ye = [go(emb_ref, xg.at[x, y, z], p) for p in yzpeers]
    xe = [[], [], []]

    def forward(v, w):
        for q, p in enumerate(xpeers):
            xe[q].append(go(xg.at[x, v, w], xg.at[x, v, w], p))

    forward(y, z)
    NL = 2
    for j, (c, (v, k)) in enumerate(zip(ye, yz_ids)):
        if j < NCB:
            turn_block(j)
        if j == NL:
            for cl in xl:
                cl.wait_recv()
            yl = [go(lg.at[y, z], lg.at[y, z], p) for p in yzpeers]
        c.wait_recv()
        forward(v, (z + NZ - k) % NZ)

    for c in yl:
        c.wait_recv()
    labs = [
        jnp.sum(lg[:, :, v].reshape(NY * NZ, 128), axis=0, keepdims=True) for v in planes
    ]
    lcol = jnp.concatenate(labs, axis=1) - base
    owned = (lcol >= 0) & (lcol < C)

    pacc = jnp.zeros((D, B), F32)
    for i in range(NCB):
        rid = lax.broadcasted_iota(jnp.int32, (CB, B), 0) + i * CB
        hot = jnp.where(rid == lcol, 1.0, 0.0).astype(BF16)
        pacc = pacc + jnp.dot(hat_t[:, i * CB : (i + 1) * CB], hot, preferred_element_type=F32)
    pt[...] = pacc.astype(BF16)
    for q in range(NX):
        psend[q] = pt[:, q * 128 : (q + 1) * 128]
    px = [go(psend.at[q + 1], precv_x.at[q], p) for q, p in enumerate(xpeers)]

    def emb_plane(q):
        e = xg[planes[q]].astype(F32)
        inv = lax.rsqrt(jnp.sum(e * e, axis=-1, keepdims=True) + EPS)
        ehat[q * 128 : (q + 1) * 128] = (e * inv).reshape(128, D).astype(BF16)

    def cos_chunk(h):
        cols = slice(h * HB, (h + 1) * HB)
        lc = lcol[:, cols]

        def score(i):
            cosb[i % 2] = lax.dot_general(
                hat[i * CB : (i + 1) * CB], ehat[cols],
                (((1,), (1,)), ((), ())), preferred_element_type=F32,
            )

        t_acc = jnp.zeros((8, HB), F32)
        score(0)
        for i in range(NCB):
            if i + 1 < NCB:
                score(i + 1)
            rid = lax.broadcasted_iota(jnp.int32, (CB, HB), 0)
            e = jnp.where(rid == lc - i * CB, 0.0, jnp.exp2(LOG2E * cosb[i % 2]))
            wt_ref[i * CB : (i + 1) * CB, cols] = e.astype(BF16)
            t_acc = t_acc + jnp.sum(e.reshape(CB // 8, 8, HB), axis=0)
        return t_acc

    def n_chunk(h):
        cols = slice(h * HB, (h + 1) * HB)
        t = jnp.dot(hat_t[...], wt_ref[:, cols], preferred_element_type=F32)
        if h == 0:
            own_n[...] = t[:, :128]
            dsend[1] = t[:, 128:].astype(BF16)
            return [go(dsend.at[1], drecv_x.at[0], xpeers[0])]
        dsend[2] = t[:, :128].astype(BF16)
        dsend[3] = t[:, 128:].astype(BF16)
        return [go(dsend.at[q], drecv_x.at[q - 1], xpeers[q - 1]) for q in (2, 3)]

    for c in xe[1]:
        c.wait_recv()
    emb_plane(0)
    emb_plane(1)
    t0 = cos_chunk(0)
    dx = n_chunk(0)
    for c in xe[0] + xe[2]:
        c.wait_recv()
    emb_plane(2)
    emb_plane(3)
    t1 = cos_chunk(1)
    t_part = jnp.sum(jnp.concatenate([t0, t1], axis=1), axis=0, keepdims=True)
    a = lax.broadcasted_iota(jnp.int32, (HB, HB), 0)
    b = lax.broadcasted_iota(jnp.int32, (HB, HB), 1)
    tc = []
    for h in range(2):
        cols = slice(h * HB, (h + 1) * HB)
        m = jnp.dot(ehat[cols], pt[:, cols], preferred_element_type=F32)
        tc.append(jnp.sum(jnp.where(a == b, m, 0.0), axis=0, keepdims=True))
    tcos = jnp.concatenate(tc, axis=1)
    tsin = jnp.sqrt(1.04 - tcos * tcos)
    shifted = tcos * MC - tsin * MS
    slope = jnp.where(owned, MC + MS * tcos / tsin, 0.0)
    et = jnp.where(owned, jnp.exp2(LOG2E * shifted), 0.0)
    t_part = t_part + et
    for q in range(NX):
        csend[0, pl.ds(planes[q], 1)] = t_part[:, q * 128 : (q + 1) * 128]
    cx = [go(csend.at[0], crecv_x.at[q], p) for q, p in enumerate(xpeers)]
    dx += n_chunk(1)
    for c in cx:
        c.wait_recv()
    csend[1] = csend[0] + crecv_x[0] + crecv_x[1] + crecv_x[2]
    cyz = [go(csend.at[1], crecv_yz.at[j], p) for j, p in enumerate(yzpeers)]
    for c in px:
        c.wait_recv()
    own = psend[0].astype(F32)
    for q in range(3):
        own = own + precv_x[q].astype(F32)
    prow[...] = own.T.reshape(NY, NZ, ROWS, D).astype(BF16)
    pyz = [
        go(prow.at[v, (z + k) % NZ], precv.at[j], p)
        for j, (p, (v, k)) in enumerate(zip(yzpeers, yz_ids))
    ]
    for c in dx:
        c.wait_recv()
    own = own_n[...]
    for q in range(3):
        own = own + drecv_x[q].astype(F32)
    rows = own.T.reshape(NY, NZ, ROWS, D)
    drow[...] = rows
    drow_b[...] = rows.astype(BF16)
    dyz = [
        go(drow_b.at[v, (z + k) % NZ], drecv.at[j], p)
        for j, (p, (v, k)) in enumerate(zip(yzpeers, yz_ids))
    ]
    for c in cyz:
        c.wait_recv()
    tot = csend[1]
    for j in range(15):
        tot = tot + crecv_yz[j]
    ctot[...] = tot

    total = jnp.concatenate([ctot[pl.ds(v, 1)] for v in planes], axis=1)
    ca = 64.0 / total
    coef = slope * (et - total)
    for k in range(4):
        cols = slice(k * 128, (k + 1) * 128)
        col = jnp.broadcast_to(ca[:, cols], (128, 128)).T
        for j in range(4):
            dcols = slice(j * 128, (j + 1) * 128)
            v = ehat[cols, dcols].astype(F32) * col
            scaled_ref[cols, dcols] = v.astype(BF16)

    coef_ref[...] = jnp.broadcast_to(coef, (8, B))
    lcol_ref[...] = jnp.broadcast_to(lcol, (8, B))
    for i in range(NK):
        out_ref[i * CB : (i + 1) * CB] = class_rows(
            i, lcol_ref, coef_ref, wt_ref, raw_ref, scaled_ref
        )
    for c in pyz:
        c.wait_recv()
    pick = prow[y, z].astype(F32)
    for j in range(15):
        pick = pick + precv[j].astype(F32)
    e = emb_ref[...].astype(F32)
    inv = lax.rsqrt(jnp.sum(e * e, axis=1, keepdims=True) + EPS)
    u = e * inv
    tc = jnp.sum(u.astype(BF16).astype(F32) * pick, axis=1, keepdims=True)
    ts = jnp.sqrt(1.04 - tc * tc)
    sh = tc * MC - ts * MS
    sl = MC + MS * tc / ts
    sub = lax.broadcasted_iota(jnp.int32, (ROWS, 128), 0)
    lan = lax.broadcasted_iota(jnp.int32, (ROWS, 128), 1)
    trow = jnp.broadcast_to(ctot[pl.ds(x, 1)], (ROWS, 128))
    tcol = jnp.sum(jnp.where(lan == sub + off, trow, 0.0), axis=1, keepdims=True)
    loss = jnp.log(tcol) - 64.0 * sh
    loss_ref[...] = jnp.sum(jnp.where(lan == sub, loss, 0.0), axis=0, keepdims=True)
    inv_t = 64.0 / tcol
    part = (sl * (jnp.exp2(LOG2E * sh) * inv_t - 64.0)) * pick
    for c in dyz:
        c.wait_recv()
    n = drow[y, z]
    for j in range(15):
        n = n + drecv[j].astype(F32)
    g = n * inv_t + part
    grad_ref[...] = inv * (g - u * jnp.sum(u * g, axis=1, keepdims=True))
    for c in pending:
        c.wait_send()


def write_kernel(
    val_ref, grad_ref, loss_ref, wt_ref, raw_ref, scaled_ref, coef_ref, lcol_ref,
    out_ref, gout_ref, lout_ref, buf, sem,
):
    copies = []

    def put(src, i):
        c = pltpu.make_async_copy(src, out_ref.at[pl.ds(i * CB, CB)], sem.at[i])
        c.start()
        copies.append(c)

    for i in range(NK):
        put(val_ref.at[pl.ds(i * CB, CB)], i)
    gout_ref[...] = grad_ref[...]
    lout_ref[...] = loss_ref[0:1, 0:ROWS]
    for i in range(NK, NCB):
        buf[i - NK] = class_rows(i, lcol_ref, coef_ref, wt_ref, raw_ref, scaled_ref)
        put(buf.at[i - NK], i)
    for c in copies:
        c.wait()


def whole(embeddings, labels, centers):
    vm = pl.BlockSpec(memory_space=pltpu.VMEM)
    hbm = pl.BlockSpec(memory_space=pltpu.HBM)
    made = pl.pallas_call(
        head_kernel,
        out_shape=(
            pltpu.VMEM((NK * CB, D), F32),
            pltpu.VMEM((ROWS, D), F32),
            pltpu.VMEM((1, 128), F32),
            pltpu.VMEM((C, B), BF16),
            pltpu.VMEM((C, D), BF16),
            pltpu.VMEM((B, D), BF16),
            pltpu.VMEM((8, B), F32),
            pltpu.VMEM((8, B), jnp.int32),
        ),
        in_specs=[hbm] * 3,
        out_specs=(vm,) * 8,
        scratch_shapes=[
            pltpu.SMEM((ROWS,), jnp.int32),
            pltpu.VMEM((ROWS, D), BF16),
            pltpu.VMEM((NX, NY, NZ, ROWS, D), BF16),
            pltpu.VMEM((NY, NZ, NX, 1, 128), jnp.int32),
            pltpu.VMEM((C, D), BF16),
            pltpu.VMEM((D, C), BF16),
            pltpu.VMEM((B, D), BF16),
            pltpu.VMEM((2, CB, HB), F32),
            pltpu.VMEM((D, 128), F32),
            pltpu.VMEM((D, B), BF16),
            pltpu.VMEM((2, NX, 128), F32),
            pltpu.VMEM((3, NX, 128), F32),
            pltpu.VMEM((15, NX, 128), F32),
            pltpu.VMEM((NX, 128), F32),
            pltpu.VMEM((NX, D, 128), BF16),
            pltpu.VMEM((3, D, 128), BF16),
            pltpu.VMEM((NY, NZ, ROWS, D), BF16),
            pltpu.VMEM((15, ROWS, D), BF16),
            pltpu.VMEM((NX, D, 128), BF16),
            pltpu.VMEM((3, D, 128), BF16),
            pltpu.VMEM((NY, NZ, ROWS, D), F32),
            pltpu.VMEM((NY, NZ, ROWS, D), BF16),
            pltpu.VMEM((15, ROWS, D), BF16),
            pltpu.SemaphoreType.DMA((NCB + 2,)),
            pltpu.SemaphoreType.DMA((140,)),
            pltpu.SemaphoreType.DMA((140,)),
        ],
        compiler_params=pltpu.CompilerParams(
            collective_id=0, has_side_effects=True, vmem_limit_bytes=48 * 1024 * 1024
        ),
        name="head",
    )(labels, embeddings, centers)
    out, grad, loss = pl.pallas_call(
        write_kernel,
        out_shape=(
            jax.ShapeDtypeStruct((C, D), F32),
            jax.ShapeDtypeStruct((ROWS, D), F32),
            jax.ShapeDtypeStruct((1, ROWS), F32),
        ),
        in_specs=[vm] * 8,
        out_specs=(pl.BlockSpec(memory_space=pltpu.HBM), vm, vm),
        scratch_shapes=[
            pltpu.VMEM((NCB - NK, CB, D), F32),
            pltpu.SemaphoreType.DMA((NCB,)),
        ],
        compiler_params=pltpu.CompilerParams(vmem_limit_bytes=12 * 1024 * 1024),
        name="write",
    )(*made)
    return loss.reshape(ROWS), grad, out


def solution(mesh):
    in_specs = (P(("dp", "cls"), None), P(("dp", "cls")), P(("dp", "cls"), None))
    out_specs = (P(("dp", "cls")), P(("dp", "cls"), None), P(("dp", "cls"), None))
    return jax.shard_map(
        whole, mesh=mesh, in_specs=in_specs, out_specs=out_specs, check_vma=False
    )
```

time: 58.1 us -> 50.3 us (0.87)
  Pallas kernels: 57.2 us -> 49.4 us
    pallas_call x1, Pallas kernels: 53.2 us -> 45.3 us  [whole(): pl.pallas_call(head_kernel, out_shape=(pltpu.VMEM((NK * CB, D), F32), plt...]
where the time goes in v3:
time: 50.3 us; the launch traced here: 50.2 us
  Pallas kernels  49.4 us (98%)
  between operations  0.8 us (2%)
    pallas_call x1, Pallas kernels, whole(): pl.pallas_call(head_kernel, out_shape=(pltpu.VMEM((NK * CB, D), F32), plt...  45.3 us
    pallas_call x1, Pallas kernels, whole(): pl.pallas_call(write_kernel, out_shape=(jax.ShapeDtypeStruct((C, D), F32)...  4.07 us

profile of v3, /device:TPU:8, one launch (start us, length us, event | category | flops | bytes accessed | tf_op | source)
XLA Modules:
  0.0 50.2 jit_solution(4869530202321734762)
XLA Ops:
  0.6 45.3 %head.1 = (f32[3072,512]{1,0:T(8,128)S(1)}, f32[8,512]{1,0:T(8,128)S(1)}, f32[1,128]{1,0:T(1,128)S(1)}, bf16[4096,512]{1,0:T(8,128)(2,1)S(1)}, bf16[4096,512]{1,...) custom-call(s32[8]{0:T(128)} %lab_hbm.1, bf16[8,512]{1,0:T(8,128)(2,1)} %emb_hbm.1, ...), custom_call_target="tpu_custom_call" | custom-call | tf_op jit(solution)/shard_map/head/pallas_call | solution.py:339
  45.9 4.1 %write.1 = (f32[4096,512]{1,0:T(8,128)}, f32[8,512]{1,0:T(8,128)}, f32[1,8]{1,0:T(1,128)}) custom-call(f32[3072,512]{1,0:T(8,128)S(1)} %get-tuple-element.14.val_ref, f32[8,512]{1,0:T(8,128)S(1)} %get-tuple-element.15.grad_ref, f32[1,128]{1,0:T(1,128)S(1)} %get-tuple-element.16.loss_ref, bf16[4096,512]{1,0:T(8,128)(2,1)S(1)} %get-tuple-element.17.wt_ref, ...), custom_call_target="tpu_custom_call" | custom-call | tf_op jit(solution)/shard_map/write/pallas_call | solution.py:386

commit v4 on v3

--- a/solution.py
+++ b/solution.py
@@ -46,7 +46,7 @@
     lab_hbm, emb_hbm, cen_ref,
     out_ref, grad_ref, loss_ref, wt_ref, raw_ref, scaled_ref, coef_ref, lcol_ref,
     lab_ref, emb_ref, xg, lg, hat, hat_t, ehat, cosb,
-    own_n, pt, csend, crecv_x, crecv_yz, ctot,
+    own_n, pt, tacc, csend, crecv_x, crecv_yz, ctot,
     psend, precv_x, prow, precv, dsend, drecv_x, drow, drow_b, drecv,
     cen_sem, send_sem, recv_sem,
 ):
@@ -65,6 +65,10 @@
     yzpeers = [pid(x, v, (z + k) % NZ) for v, k in yz_ids]
     base = me * C
 
+    barrier = pltpu.get_barrier_semaphore()
+    for p in yzpeers + xpeers:
+        pl.semaphore_signal(barrier, inc=1, device_id={"cls": p})
+
     def cen_copy(i):
         rows = pl.ds(i * CB, CB)
         return pltpu.make_async_copy(cen_ref.at[rows], raw_ref.at[rows], cen_sem.at[i])
@@ -77,10 +81,6 @@
         c.start()
     for i in range(NCB):
         cen_copy(i).start()
-
-    barrier = pltpu.get_barrier_semaphore()
-    for p in yzpeers + xpeers:
-        pl.semaphore_signal(barrier, inc=1, device_id={"cls": p})
 
     lane = lax.broadcasted_iota(jnp.int32, (1, 128), 1)
     off = (y * NZ + z) * ROWS
@@ -101,14 +101,11 @@
 
     def turn_block(i):
         rows = pl.ds(i * CB, CB)
-        a = lax.broadcasted_iota(jnp.int32, (D, D), 0)
-        b = lax.broadcasted_iota(jnp.int32, (D, D), 1)
-        eye = jnp.where(a == b, 1.0, 0.0).astype(BF16)
-        t = lax.dot_general(eye, hat[rows], (((1,), (1,)), ((), ())), preferred_element_type=F32)
-        hat_t[:, rows] = t.astype(BF16)
-
-    for i in range(NCB):
-        norm_block(i)
+        hat_t[:, rows] = hat[rows].T
+
+    def apart(body):
+        pl.when(me >= 0)(body)
+
     pl.semaphore_wait(barrier, 18)
 
     pending = []
@@ -135,7 +132,9 @@
             xe[q].append(go(xg.at[x, v, w], xg.at[x, v, w], p))
 
     forward(y, z)
-    NL = 2
+    for i in range(NCB):
+        norm_block(i)
+    NL = 4
     for j, (c, (v, k)) in enumerate(zip(ye, yz_ids)):
         if j < NCB:
             turn_block(j)
@@ -154,14 +153,20 @@
     lcol = jnp.concatenate(labs, axis=1) - base
     owned = (lcol >= 0) & (lcol < C)
 
-    pacc = jnp.zeros((D, B), F32)
-    for i in range(NCB):
-        rid = lax.broadcasted_iota(jnp.int32, (CB, B), 0) + i * CB
-        hot = jnp.where(rid == lcol, 1.0, 0.0).astype(BF16)
-        pacc = pacc + jnp.dot(hat_t[:, i * CB : (i + 1) * CB], hot, preferred_element_type=F32)
-    pt[...] = pacc.astype(BF16)
-    for q in range(NX):
-        psend[q] = pt[:, q * 128 : (q + 1) * 128]
+    def pick_labels():
+        acc = jnp.zeros((D, B), F32)
+        for i in range(NCB):
+            rid = lax.broadcasted_iota(jnp.int32, (CB, B), 0) + i * CB
+            hot = jnp.where(rid == lcol, 1.0, 0.0).astype(BF16)
+            acc = acc + jnp.dot(
+                hat_t[:, i * CB : (i + 1) * CB], hot, preferred_element_type=F32
+            )
+        p = acc.astype(BF16)
+        pt[...] = p
+        for q in range(NX):
+            psend[q] = p[:, q * 128 : (q + 1) * 128]
+
+    apart(pick_labels)
     px = [go(psend.at[q + 1], precv_x.at[q], p) for q, p in enumerate(xpeers)]
 
     def emb_plane(q):
@@ -188,31 +193,33 @@
             e = jnp.where(rid == lc - i * CB, 0.0, jnp.exp2(LOG2E * cosb[i % 2]))
             wt_ref[i * CB : (i + 1) * CB, cols] = e.astype(BF16)
             t_acc = t_acc + jnp.sum(e.reshape(CB // 8, 8, HB), axis=0)
-        return t_acc
+        tacc[:, cols] = t_acc
 
     def n_chunk(h):
         cols = slice(h * HB, (h + 1) * HB)
         t = jnp.dot(hat_t[...], wt_ref[:, cols], preferred_element_type=F32)
         if h == 0:
             own_n[...] = t[:, :128]
-            dsend[1] = t[:, 128:].astype(BF16)
-            return [go(dsend.at[1], drecv_x.at[0], xpeers[0])]
-        dsend[2] = t[:, :128].astype(BF16)
-        dsend[3] = t[:, 128:].astype(BF16)
-        return [go(dsend.at[q], drecv_x.at[q - 1], xpeers[q - 1]) for q in (2, 3)]
+        else:
+            dsend[2] = t[:, :128].astype(BF16)
+        dsend[2 * h + 1] = t[:, 128:].astype(BF16)
+
+    def n_send(q):
+        return go(dsend.at[q], drecv_x.at[q - 1], xpeers[q - 1])
 
     for c in xe[1]:
         c.wait_recv()
     emb_plane(0)
     emb_plane(1)
-    t0 = cos_chunk(0)
-    dx = n_chunk(0)
+    apart(lambda: cos_chunk(0))
+    apart(lambda: n_chunk(0))
+    dx = [n_send(1)]
     for c in xe[0] + xe[2]:
         c.wait_recv()
     emb_plane(2)
     emb_plane(3)
-    t1 = cos_chunk(1)
-    t_part = jnp.sum(jnp.concatenate([t0, t1], axis=1), axis=0, keepdims=True)
+    apart(lambda: cos_chunk(1))
+    t_part = jnp.sum(tacc[...], axis=0, keepdims=True)
     a = lax.broadcasted_iota(jnp.int32, (HB, HB), 0)
     b = lax.broadcasted_iota(jnp.int32, (HB, HB), 1)
     tc = []
@@ -229,7 +236,8 @@
     for q in range(NX):
         csend[0, pl.ds(planes[q], 1)] = t_part[:, q * 128 : (q + 1) * 128]
     cx = [go(csend.at[0], crecv_x.at[q], p) for q, p in enumerate(xpeers)]
-    dx += n_chunk(1)
+    apart(lambda: n_chunk(1))
+    dx += [n_send(2), n_send(3)]
     for c in cx:
         c.wait_recv()
     csend[1] = csend[0] + crecv_x[0] + crecv_x[1] + crecv_x[2]
@@ -276,10 +284,14 @@
 
     coef_ref[...] = jnp.broadcast_to(coef, (8, B))
     lcol_ref[...] = jnp.broadcast_to(lcol, (8, B))
-    for i in range(NK):
+
+    def class_block(i):
         out_ref[i * CB : (i + 1) * CB] = class_rows(
             i, lcol_ref, coef_ref, wt_ref, raw_ref, scaled_ref
         )
+
+    for i in range(NK):
+        apart(functools.partial(class_block, i))
     for c in pyz:
         c.wait_recv()
     pick = prow[y, z].astype(F32)
@@ -361,6 +373,7 @@
             pltpu.VMEM((2, CB, HB), F32),
             pltpu.VMEM((D, 128), F32),
             pltpu.VMEM((D, B), BF16),
+            pltpu.VMEM((8, B), F32),
             pltpu.VMEM((2, NX, 128), F32),
             pltpu.VMEM((3, NX, 128), F32),
             pltpu.VMEM((15, NX, 128), F32),

time: 50.3 us -> 48.4 us (0.962)
  the two profiles are of different devices: /device:TPU:8 before, /device:TPU:6 now
where the time goes in v4:
time: 48.4 us; the launch traced here: 48.3 us
  Pallas kernels  47.5 us (98%)
  between operations  0.8 us (2%)
    pallas_call x1, Pallas kernels, whole(): pl.pallas_call(head_kernel, out_shape=(pltpu.VMEM((NK * CB, D), F32), plt...  43.5 us
    pallas_call x1, Pallas kernels, whole(): pl.pallas_call(write_kernel, out_shape=(jax.ShapeDtypeStruct((C, D), F32)...  4.08 us

profile of v4, /device:TPU:6, one launch (start us, length us, event | category | flops | bytes accessed | tf_op | source)
XLA Modules:
  0.0 48.3 jit_solution(6827956825441395440)
XLA Ops:
  0.6 43.5 %head.1 = (f32[3072,512]{1,0:T(8,128)S(1)}, f32[8,512]{1,0:T(8,128)S(1)}, f32[1,128]{1,0:T(1,128)S(1)}, bf16[4096,512]{1,0:T(8,128)(2,1)S(1)}, bf16[4096,512]{1,...) custom-call(s32[8]{0:T(128)} %lab_hbm.1, bf16[8,512]{1,0:T(8,128)(2,1)} %emb_hbm.1, ...), custom_call_target="tpu_custom_call" | custom-call | tf_op jit(solution)/shard_map/head/pallas_call | solution.py:351
  44.1 4.1 %write.1 = (f32[4096,512]{1,0:T(8,128)}, f32[8,512]{1,0:T(8,128)}, f32[1,8]{1,0:T(1,128)}) custom-call(f32[3072,512]{1,0:T(8,128)S(1)} %get-tuple-element.14.val_ref, f32[8,512]{1,0:T(8,128)S(1)} %get-tuple-element.15.grad_ref, f32[1,128]{1,0:T(1,128)S(1)} %get-tuple-element.16.loss_ref, bf16[4096,512]{1,0:T(8,128)(2,1)S(1)} %get-tuple-element.17.wt_ref, ...), custom_call_target="tpu_custom_call" | custom-call | tf_op jit(solution)/shard_map/write/pallas_call | solution.py:399

commit v5 on v4

v5 whole, which is shorter than its diff:
```python
import functools
import math

import jax
import jax.numpy as jnp
from jax import lax
from jax.experimental import pallas as pl
from jax.experimental.pallas import tpu as pltpu
from jax.sharding import PartitionSpec as P

MC = math.cos(0.5)
MS = math.sin(0.5)
EPS = 1e-06
NX, NY, NZ = 4, 2, 8
ROWS = 8
D = 512
C = 4096
B = 512
CB = 512
NCB = C // CB
F32 = jnp.float32
BF16 = jnp.bfloat16
ZOFF = (0, 1, 7, 2, 6, 3, 5, 4)
XY = ((1, 0), (3, 0), (2, 0), (0, 1), (1, 1), (3, 1), (2, 1))
HB = B // 2
NK = 7
LOG2E = 64.0 / math.log(2.0)


def pid(x, y, z):
    return x * (NY * NZ) + z * NY + y


def class_rows(i, lcol_ref, coef_ref, wt_ref, raw_ref, scaled_ref):
    rows = slice(i * CB, (i + 1) * CB)
    rid = lax.broadcasted_iota(jnp.int32, (CB, B), 0) + i * CB
    w = jnp.where(rid == lcol_ref[0:1], coef_ref[0:1], wt_ref[rows].astype(F32)).astype(BF16)
    g = jnp.dot(w, scaled_ref[...], preferred_element_type=F32)
    v = raw_ref[rows].astype(F32)
    inv = lax.rsqrt(jnp.sum(v * v, axis=1, keepdims=True) + EPS)
    dot = jnp.sum(v * g, axis=1, keepdims=True)
    return inv * g - (inv * inv * inv * dot) * v


def head_kernel(
    lab_hbm, emb_hbm, cen_ref,
    out_ref, grad_ref, loss_ref, wt_ref, raw_ref, scaled_ref, coef_ref, lcol_ref,
    lab_ref, emb_ref, xg, lg, hat, hat_t, ehat, cosb, lcolb, tacc,
    csend, crecv_xy, crecv_z, ctot,
    psend, precv_y, psum, precv_x, pz, precv_z,
    nsend, nown, nrecv, nz, nz_b, nrecv_z,
    cen_sem, send_sem, recv_sem,
):
    me = lax.axis_index("cls")
    x = me // (NY * NZ)
    z = (me % (NY * NZ)) // NY
    y = me % NY
    ys = (y, 1 - y)
    xk = {k: (x + k) % NX for k in range(NX)}
    zpeers = [pid(x, y, (z + k) % NZ) for k in ZOFF[1:]]
    ypeer = pid(x, ys[1], z)
    xypeers = [pid(xk[k], ys[h], z) for k, h in XY]
    base = me * C

    barrier = pltpu.get_barrier_semaphore()
    for p in zpeers + xypeers:
        pl.semaphore_signal(barrier, inc=1, device_id={"cls": p})

    def cen_copy(i):
        rows = pl.ds(i * CB, CB)
        return pltpu.make_async_copy(cen_ref.at[rows], raw_ref.at[rows], cen_sem.at[i])

    small = [
        pltpu.make_async_copy(lab_hbm, lab_ref, cen_sem.at[NCB]),
        pltpu.make_async_copy(emb_hbm, emb_ref, cen_sem.at[NCB + 1]),
    ]
    for c in small:
        c.start()
    for i in range(NCB):
        cen_copy(i).start()

    lane = lax.broadcasted_iota(jnp.int32, (1, 128), 1)
    off = (x % 2) * 64 + z * ROWS
    lrow = jnp.zeros((1, 128), jnp.int32)
    for c in small:
        c.wait()
    for r in range(ROWS):
        lrow = jnp.where(lane == off + r, lab_ref[r], lrow)
    lg[y, x, z] = lrow
    xg[y, x, z] = emb_ref[...]

    def norm_block(i):
        cen_copy(i).wait()
        rows = pl.ds(i * CB, CB)
        v = raw_ref[rows].astype(F32)
        inv = lax.rsqrt(jnp.sum(v * v, axis=1, keepdims=True) + EPS)
        hat[rows] = (v * inv).astype(BF16)

    def turn_block(i):
        rows = pl.ds(i * CB, CB)
        hat_t[:, rows] = hat[rows].T

    def apart(body):
        pl.when(me >= 0)(body)

    pl.semaphore_wait(barrier, 14)

    pending = []
    nsem = [0]

    def go(src, dst, peer):
        i = nsem[0]
        nsem[0] += 1
        c = pltpu.make_async_remote_copy(
            src_ref=src, dst_ref=dst, send_sem=send_sem.at[i], recv_sem=recv_sem.at[i],
            device_id={"cls": peer},
        )
        c.start()
        pending.append(c)
        return c

    lsl = lg.at[y, x, z]
    lz = [go(lsl, lsl, p) for p in zpeers]
    ez = [go(emb_ref, xg.at[y, x, z], p) for p in zpeers]
    xf = {}
    yf = {}
    xg2 = {}

    def zat(j):
        return (z + NZ - ZOFF[j]) % NZ

    def forward_x(j):
        blk = xg.at[y, x, zat(j)]
        for k in (1, 3, 2):
            xf[j, k] = go(blk, blk, pid(xk[k], y, z))

    def forward_y(k, j):
        blk = xg.at[y, (x + NX - k) % NX, zat(j)]
        yf[k, j] = go(blk, blk, ypeer)

    def on_y(j):
        yf[0, j].wait_recv()
        blk = xg.at[ys[1], x, zat(j)]
        for k in (1, 3):
            xg2[k, j] = go(blk, blk, pid(xk[k], y, z))

    forward_x(0)
    forward_y(0, 0)

    work = [functools.partial(norm_block, i) for i in range(NCB)]
    work += [functools.partial(turn_block, i) for i in range(NCB)]

    def do(n):
        for _ in range(min(n, len(work))):
            work.pop(0)()

    def on_z(j):
        ez[j - 1].wait_recv()
        forward_x(j)
        forward_y(0, j)

    def on_x(j):
        for k in (1, 3, 2):
            xf[j, k].wait_recv()
            if k == 2:
                forward_y(k, j)

    do(4)
    on_z(1)
    on_z(2)
    do(2)
    on_z(3)
    on_z(4)
    do(2)
    on_x(0)
    on_z(5)
    on_z(6)
    do(1)
    on_z(7)
    for c in lz:
        c.wait_recv()
    lxy = [go(lg.at[y, x], lg.at[y, x], p) for p in xypeers]
    for j in range(1, NZ):
        do(1)
        on_y(j - 1)
        on_x(j)
    do(NCB)
    on_y(NZ - 1)

    def lab_half(h):
        return [
            jnp.sum(lg[ys[h], 2 * p : 2 * p + 2].reshape(2 * NZ, 128), axis=0, keepdims=True)
            - base
            for p in range(2)
        ]

    for c in lxy[:3]:
        c.wait_recv()
    labs = lab_half(0)
    lcols = [jnp.concatenate(labs, axis=1)]

    for c in lxy[3:]:
        c.wait_recv()
    labs += lab_half(1)
    lcols.append(jnp.concatenate(labs[2:], axis=1))
    lcol = jnp.concatenate(labs, axis=1)
    owned = (lcol >= 0) & (lcol < C)
    for q in range(4):
        lcolb[q * 128 : (q + 1) * 128] = jnp.broadcast_to(labs[q].astype(F32), (128, 128)).T

    def send_py(k):
        return go(psend.at[1, xk[k]], precv_y.at[xk[k]], ypeer)

    px = []

    def take_py(k):
        py[k].wait_recv()
        v = psend[0, xk[k]].astype(F32) + precv_y[xk[k]].astype(F32)
        psum[xk[k]] = v.astype(BF16)
        if k:
            px.append(go(psum.at[xk[k]], precv_x.at[k - 1], pid(xk[k], y, z)))

    def pick_labels():
        acc = jnp.zeros((B, D), F32)
        lanef = lax.broadcasted_iota(jnp.int32, (1, 128), 1).astype(F32)
        for i in range(NCB):
            hot = jnp.concatenate(
                [
                    jnp.where(lcolb[...] == lanef + float(i * CB + g * 128), 1.0, 0.0)
                    for g in range(CB // 128)
                ],
                axis=1,
            ).astype(BF16)
            acc = acc + jnp.dot(
                hot, hat[i * CB : (i + 1) * CB], preferred_element_type=F32
            )
        psend[...] = acc.astype(BF16).reshape(2, NX, 64, D)

    apart(pick_labels)
    py = {k: send_py(k) for k in (2, 1, 3)}

    def emb_half(h):
        e = xg[ys[h]].astype(F32)
        inv = lax.rsqrt(jnp.sum(e * e, axis=-1, keepdims=True) + EPS)
        ehat[h * HB : (h + 1) * HB] = (e * inv).reshape(HB, D).astype(BF16)

    def cos_chunk(h):
        cols = slice(h * HB, (h + 1) * HB)
        lc = lcols[h]

        def score(i):
            cosb[i % 2] = lax.dot_general(
                hat[i * CB : (i + 1) * CB], ehat[cols],
                (((1,), (1,)), ((), ())), preferred_element_type=F32,
            )

        t_acc = jnp.zeros((8, HB), F32)
        score(0)
        for i in range(NCB):
            if i + 1 < NCB:
                score(i + 1)
            rid = lax.broadcasted_iota(jnp.int32, (CB, HB), 0)
            e = jnp.where(rid == lc - i * CB, 0.0, jnp.exp2(LOG2E * cosb[i % 2]))
            wt_ref[i * CB : (i + 1) * CB, cols] = e.astype(BF16)
            t_acc = t_acc + jnp.sum(e.reshape(CB // 8, 8, HB), axis=0)
        tacc[:, cols] = t_acc

    def n_chunk(h):
        cols = slice(h * HB, (h + 1) * HB)
        t = jnp.dot(hat_t[...], wt_ref[:, cols], preferred_element_type=F32)
        t = t.T.reshape(NX, 64, D)
        nsend[h] = t.astype(BF16)
        if h == 0:
            nown[...] = t

    def n_send(hh):
        return [
            go(nsend.at[h, xk[k]], nrecv.at[i], xypeers[i])
            for i, (k, h) in enumerate(XY)
            if h == hh
        ]

    emb_half(0)
    apart(lambda: cos_chunk(0))
    for j in range(NZ):
        yf[2, j].wait_recv()
        xg2[1, j].wait_recv()
        xg2[3, j].wait_recv()
    emb_half(1)
    apart(lambda: cos_chunk(1))
    t_part = jnp.sum(tacc[...], axis=0, keepdims=True)
    a = lax.broadcasted_iota(jnp.int32, (HB, HB), 0)
    b = lax.broadcasted_iota(jnp.int32, (HB, HB), 1)
    tc = []
    for h in range(2):
        m = lax.dot_general(
            ehat[h * HB : (h + 1) * HB], psend[h].reshape(HB, D),
            (((1,), (1,)), ((), ())), preferred_element_type=F32,
        )
        tc.append(jnp.sum(jnp.where(a == b, m, 0.0), axis=0, keepdims=True))
    tcos = jnp.concatenate(tc, axis=1)
    tsin = jnp.sqrt(1.04 - tcos * tcos)
    shifted = tcos * MC - tsin * MS
    slope = jnp.where(owned, MC + MS * tcos / tsin, 0.0)
    et = jnp.where(owned, jnp.exp2(LOG2E * shifted), 0.0)
    t_part = t_part + et
    where_t = [ys[0] * 2, ys[0] * 2 + 1, ys[1] * 2, ys[1] * 2 + 1]
    for q in range(4):
        csend[0, pl.ds(where_t[q], 1)] = t_part[:, q * 128 : (q + 1) * 128]
    cxy = [go(csend.at[0], crecv_xy.at[i], p) for i, p in enumerate(xypeers)]
    py[0] = send_py(0)
    take_py(2)
    apart(lambda: n_chunk(1))
    nx = n_send(1)
    take_py(1)
    apart(lambda: n_chunk(0))
    nx += n_send(0)
    take_py(3)
    for c in cxy:
        c.wait_recv()
    tot = csend[0]
    for i in range(7):
        tot = tot + crecv_xy[i]
    csend[1] = tot
    cz = [go(csend.at[1], crecv_z.at[i], p) for i, p in enumerate(zpeers)]
    take_py(0)
    for c in px:
        c.wait_recv()
    s = psum[x].astype(F32)
    for i in range(3):
        s = s + precv_x[i].astype(F32)
    pz[...] = s.astype(BF16).reshape(NZ, ROWS, D)
    pzc = [
        go(pz.at[(z + k) % NZ], precv_z.at[i], p)
        for i, (k, p) in enumerate(zip(ZOFF[1:], zpeers))
    ]
    for c in nx:
        c.wait_recv()
    s = nown[x]
    for i in range(7):
        s = s + nrecv[i].astype(F32)
    s = s.reshape(NZ, ROWS, D)
    nz[...] = s
    nz_b[...] = s.astype(BF16)
    nzc = [
        go(nz_b.at[(z + k) % NZ], nrecv_z.at[i], p)
        for i, (k, p) in enumerate(zip(ZOFF[1:], zpeers))
    ]
    for c in cz:
        c.wait_recv()
    tot = csend[1]
    for i in range(7):
        tot = tot + crecv_z[i]
    ctot[...] = tot

    total = jnp.concatenate([ctot[pl.ds(v, 1)] for v in where_t], axis=1)
    ca = 64.0 / total
    coef = slope * (et - total)
    for k in range(4):
        cols = slice(k * 128, (k + 1) * 128)
        col = jnp.broadcast_to(ca[:, cols], (128, 128)).T
        for j in range(4):
            dcols = slice(j * 128, (j + 1) * 128)
            v = ehat[cols, dcols].astype(F32) * col
            scaled_ref[cols, dcols] = v.astype(BF16)
    coef_ref[...] = jnp.broadcast_to(coef, (8, B))
    lcol_ref[...] = jnp.broadcast_to(lcol, (8, B))

    def class_block(i):
        out_ref[i * CB : (i + 1) * CB] = class_rows(
            i, lcol_ref, coef_ref, wt_ref, raw_ref, scaled_ref
        )

    for i in range(NK):
        apart(functools.partial(class_block, i))
    for c in pzc:
        c.wait_recv()
    pick = pz[z].astype(F32)
    for i in range(7):
        pick = pick + precv_z[i].astype(F32)
    e = emb_ref[...].astype(F32)
    inv = lax.rsqrt(jnp.sum(e * e, axis=1, keepdims=True) + EPS)
    u = e * inv
    tc = jnp.sum(u.astype(BF16).astype(F32) * pick, axis=1, keepdims=True)
    ts = jnp.sqrt(1.04 - tc * tc)
    sh = tc * MC - ts * MS
    sl = MC + MS * tc / ts
    sub = lax.broadcasted_iota(jnp.int32, (ROWS, 128), 0)
    lan = lax.broadcasted_iota(jnp.int32, (ROWS, 128), 1)
    trow = jnp.broadcast_to(ctot[pl.ds(y * 2 + x // 2, 1)], (ROWS, 128))
    tcol = jnp.sum(jnp.where(lan == sub + off, trow, 0.0), axis=1, keepdims=True)
    loss = jnp.log(tcol) - 64.0 * sh
    loss_ref[...] = jnp.sum(jnp.where(lan == sub, loss, 0.0), axis=0, keepdims=True)
    inv_t = 64.0 / tcol
    part = (sl * (jnp.exp2(LOG2E * sh) * inv_t - 64.0)) * pick
    for c in nzc:
        c.wait_recv()
    n = nz[z]
    for i in range(7):
        n = n + nrecv_z[i].astype(F32)
    g = n * inv_t + part
    grad_ref[...] = inv * (g - u * jnp.sum(u * g, axis=1, keepdims=True))
    for c in pending:
        c.wait_send()


def write_kernel(
    val_ref, grad_ref, loss_ref, wt_ref, raw_ref, scaled_ref, coef_ref, lcol_ref,
    out_ref, gout_ref, lout_ref, buf, lbuf, sem,
):
    copies = []

    def put(src, i):
        c = pltpu.make_async_copy(src, out_ref.at[pl.ds(i * CB, CB)], sem.at[i])
        c.start()
        copies.append(c)

    for i in range(NK):
        put(val_ref.at[pl.ds(i * CB, CB)], i)
    lbuf[...] = loss_ref[0:1, 0:ROWS]
    copies.append(pltpu.make_async_copy(grad_ref, gout_ref, sem.at[NCB]))
    copies.append(pltpu.make_async_copy(lbuf, lout_ref, sem.at[NCB + 1]))
    for c in copies[NK:]:
        c.start()
    for i in range(NK, NCB):
        buf[i - NK] = class_rows(i, lcol_ref, coef_ref, wt_ref, raw_ref, scaled_ref)
        put(buf.at[i - NK], i)
    for c in copies:
        c.wait()


def whole(embeddings, labels, centers):
    vm = pl.BlockSpec(memory_space=pltpu.VMEM)
    hbm = pl.BlockSpec(memory_space=pltpu.HBM)
    made = pl.pallas_call(
        head_kernel,
        out_shape=(
            pltpu.VMEM((NK * CB, D), F32),
            pltpu.VMEM((ROWS, D), F32),
            pltpu.VMEM((1, 128), F32),
            pltpu.VMEM((C, B), BF16),
            pltpu.VMEM((C, D), BF16),
            pltpu.VMEM((B, D), BF16),
            pltpu.VMEM((8, B), F32),
            pltpu.VMEM((8, B), jnp.int32),
        ),
        in_specs=[hbm] * 3,
        out_specs=(vm,) * 8,
        scratch_shapes=[
            pltpu.SMEM((ROWS,), jnp.int32),
            pltpu.VMEM((ROWS, D), BF16),
            pltpu.VMEM((NY, NX, NZ, ROWS, D), BF16),
            pltpu.VMEM((NY, NX, NZ, 1, 128), jnp.int32),
            pltpu.VMEM((C, D), BF16),
            pltpu.VMEM((D, C), BF16),
            pltpu.VMEM((B, D), BF16),
            pltpu.VMEM((2, CB, HB), F32),
            pltpu.VMEM((B, 128), F32),
            pltpu.VMEM((8, B), F32),
            pltpu.VMEM((2, 4, 128), F32),
            pltpu.VMEM((7, 4, 128), F32),
            pltpu.VMEM((7, 4, 128), F32),
            pltpu.VMEM((4, 128), F32),
            pltpu.VMEM((2, NX, 64, D), BF16),
            pltpu.VMEM((NX, 64, D), BF16),
            pltpu.VMEM((NX, 64, D), BF16),
            pltpu.VMEM((3, 64, D), BF16),
            pltpu.VMEM((NZ, ROWS, D), BF16),
            pltpu.VMEM((7, ROWS, D), BF16),
            pltpu.VMEM((2, NX, 64, D), BF16),
            pltpu.VMEM((NX, 64, D), F32),
            pltpu.VMEM((7, 64, D), BF16),
            pltpu.VMEM((NZ, ROWS, D), F32),
            pltpu.VMEM((NZ, ROWS, D), BF16),
            pltpu.VMEM((7, ROWS, D), BF16),
            pltpu.SemaphoreType.DMA((NCB + 2,)),
            pltpu.SemaphoreType.DMA((130,)),
            pltpu.SemaphoreType.DMA((130,)),
        ],
        compiler_params=pltpu.CompilerParams(
            collective_id=0, has_side_effects=True, vmem_limit_bytes=48 * 1024 * 1024
        ),
        name="head",
    )(labels, embeddings, centers)
    out, grad, loss = pl.pallas_call(
        write_kernel,
        out_shape=(
            jax.ShapeDtypeStruct((C, D), F32),
            jax.ShapeDtypeStruct((ROWS, D), F32),
            jax.ShapeDtypeStruct((1, ROWS), F32),
        ),
        in_specs=[vm] * 8,
        out_specs=(hbm,) * 3,
        scratch_shapes=[
            pltpu.VMEM((NCB - NK, CB, D), F32),
            pltpu.VMEM((1, ROWS), F32),
            pltpu.SemaphoreType.DMA((NCB + 2,)),
        ],
        compiler_params=pltpu.CompilerParams(vmem_limit_bytes=12 * 1024 * 1024),
        name="write",
    )(*made)
    return loss.reshape(ROWS), grad, out


def solution(mesh):
    in_specs = (P(("dp", "cls"), None), P(("dp", "cls")), P(("dp", "cls"), None))
    out_specs = (P(("dp", "cls")), P(("dp", "cls"), None), P(("dp", "cls"), None))
    return jax.shard_map(
        whole, mesh=mesh, in_specs=in_specs, out_specs=out_specs, check_vma=False
    )
```

time: 48.4 us -> 46.3 us (0.957)
  the two profiles are of different devices: /device:TPU:6 before, /device:TPU:8 now
where the time goes in v5:
time: 46.3 us; the launch traced here: 46.2 us
  Pallas kernels  45.4 us (98%)
  between operations  0.8 us (2%)
    pallas_call x1, Pallas kernels, whole(): pl.pallas_call(head_kernel, out_shape=(pltpu.VMEM((NK * CB, D), F32), plt...  42 us
    pallas_call x1, Pallas kernels, whole(): pl.pallas_call(write_kernel, out_shape=(jax.ShapeDtypeStruct((C, D), F32)...  3.41 us

profile of v5, /device:TPU:8, one launch (start us, length us, event | category | flops | bytes accessed | tf_op | source)
XLA Modules:
  0.0 46.2 jit_solution(7858436321299945583)
XLA Ops:
  0.6 42.0 %head.1 = (f32[3584,512]{1,0:T(8,128)S(1)}, f32[8,512]{1,0:T(8,128)S(1)}, f32[1,128]{1,0:T(1,128)S(1)}, bf16[4096,512]{1,0:T(8,128)(2,1)S(1)}, bf16[4096,512]{1,...) custom-call(s32[8]{0:T(128)} %lab_hbm.1, bf16[8,512]{1,0:T(8,128)(2,1)} %emb_hbm.1, ...), custom_call_target="tpu_custom_call" | custom-call | tf_op jit(solution)/shard_map/head/pallas_call | solution.py:435
  42.7 3.4 %write.1 = (f32[4096,512]{1,0:T(8,128)}, f32[8,512]{1,0:T(8,128)}, f32[1,8]{1,0:T(1,128)}) custom-call(f32[3584,512]{1,0:T(8,128)S(1)} %get-tuple-element.14.val_ref, f32[8,512]{1,0:T(8,128)S(1)} %get-tuple-element.15.grad_ref, f32[1,128]{1,0:T(1,128)S(1)} %get-tuple-element.16.loss_ref, bf16[4096,512]{1,0:T(8,128)(2,1)S(1)} %get-tuple-element.17.wt_ref, ...), custom_call_target="tpu_custom_call" | custom-call | tf_op jit(solution)/shard_map/write/pallas_call | solution.py:485

commit v6 on v5

--- a/solution.py
+++ b/solution.py
@@ -23,7 +23,7 @@
 ZOFF = (0, 1, 7, 2, 6, 3, 5, 4)
 XY = ((1, 0), (3, 0), (2, 0), (0, 1), (1, 1), (3, 1), (2, 1))
 HB = B // 2
-NK = 7
+NK = 6
 LOG2E = 64.0 / math.log(2.0)
 
 
@@ -47,8 +47,8 @@
     out_ref, grad_ref, loss_ref, wt_ref, raw_ref, scaled_ref, coef_ref, lcol_ref,
     lab_ref, emb_ref, xg, lg, hat, hat_t, ehat, cosb, lcolb, tacc,
     csend, crecv_xy, crecv_z, ctot,
-    psend, precv_y, psum, precv_x, pz, precv_z,
-    nsend, nown, nrecv, nz, nz_b, nrecv_z,
+    psend, precv_y, precv_x13, psum, precv_x, pz, precv_z,
+    nsend, nown, nrecv_a, nmid, nrecv, nz, nz_b, nrecv_z,
     cen_sem, send_sem, recv_sem,
 ):
     me = lax.axis_index("cls")
@@ -105,26 +105,33 @@
 
     pl.semaphore_wait(barrier, 14)
 
-    pending = []
-    nsem = [0]
-
-    def go(src, dst, peer):
-        i = nsem[0]
-        nsem[0] += 1
-        c = pltpu.make_async_remote_copy(
-            src_ref=src, dst_ref=dst, send_sem=send_sem.at[i], recv_sem=recv_sem.at[i],
+    groups = []
+    sent = []
+
+    def group():
+        groups.append(None)
+        return len(groups) - 1
+
+    def go(src, dst, peer, g):
+        pltpu.make_async_remote_copy(
+            src_ref=src, dst_ref=dst, send_sem=send_sem.at[0], recv_sem=recv_sem.at[g],
             device_id={"cls": peer},
-        )
-        c.start()
-        pending.append(c)
-        return c
+        ).start()
+
+    def arrive(g, ref):
+        pltpu.make_async_copy(ref, ref, recv_sem.at[g]).wait()
+        sent.append(ref)
 
     lsl = lg.at[y, x, z]
-    lz = [go(lsl, lsl, p) for p in zpeers]
-    ez = [go(emb_ref, xg.at[y, x, z], p) for p in zpeers]
-    xf = {}
-    yf = {}
-    xg2 = {}
+    lz = group()
+    for p in zpeers:
+        go(lsl, lsl, p, lz)
+    ez = [group() for p in zpeers]
+    for g, p in zip(ez, zpeers):
+        go(emb_ref, xg.at[y, x, z], p, g)
+    xf = [group() for j in range(NZ)]
+    yf = [group() for j in range(NZ)]
+    rest = group()
 
     def zat(j):
         return (z + NZ - ZOFF[j]) % NZ
@@ -132,59 +139,52 @@
     def forward_x(j):
         blk = xg.at[y, x, zat(j)]
         for k in (1, 3, 2):
-            xf[j, k] = go(blk, blk, pid(xk[k], y, z))
+            go(blk, blk, pid(xk[k], y, z), xf[j])
 
     def forward_y(k, j):
         blk = xg.at[y, (x + NX - k) % NX, zat(j)]
-        yf[k, j] = go(blk, blk, ypeer)
+        go(blk, blk, ypeer, rest if k else yf[j])
 
     def on_y(j):
-        yf[0, j].wait_recv()
+        arrive(yf[j], emb_ref)
         blk = xg.at[ys[1], x, zat(j)]
         for k in (1, 3):
-            xg2[k, j] = go(blk, blk, pid(xk[k], y, z))
+            go(blk, blk, pid(xk[k], y, z), rest)
 
     forward_x(0)
     forward_y(0, 0)
 
     work = [functools.partial(norm_block, i) for i in range(NCB)]
-    work += [functools.partial(turn_block, i) for i in range(NCB)]
 
     def do(n):
         for _ in range(min(n, len(work))):
             work.pop(0)()
 
     def on_z(j):
-        ez[j - 1].wait_recv()
+        arrive(ez[j - 1], emb_ref)
         forward_x(j)
         forward_y(0, j)
 
     def on_x(j):
-        for k in (1, 3, 2):
-            xf[j, k].wait_recv()
-            if k == 2:
-                forward_y(k, j)
-
-    do(4)
+        arrive(xf[j], xg.at[y, x, pl.ds(0, 3)])
+        forward_y(2, j)
+
+    do(NCB)
     on_z(1)
     on_z(2)
-    do(2)
     on_z(3)
     on_z(4)
-    do(2)
     on_x(0)
     on_z(5)
     on_z(6)
-    do(1)
     on_z(7)
-    for c in lz:
-        c.wait_recv()
-    lxy = [go(lg.at[y, x], lg.at[y, x], p) for p in xypeers]
+    arrive(lz, lg.at[y, x, pl.ds(0, 7)])
+    lxy = [group(), group()]
+    for i, p in enumerate(xypeers):
+        go(lg.at[y, x], lg.at[y, x], p, lxy[min(i // 3, 1)])
     for j in range(1, NZ):
-        do(1)
+        on_x(j)
         on_y(j - 1)
-        on_x(j)
-    do(NCB)
     on_y(NZ - 1)
 
     def lab_half(h):
@@ -194,13 +194,11 @@
             for p in range(2)
         ]
 
-    for c in lxy[:3]:
-        c.wait_recv()
+    arrive(lxy[0], lg.at[y, pl.ds(0, 3)])
     labs = lab_half(0)
     lcols = [jnp.concatenate(labs, axis=1)]
 
-    for c in lxy[3:]:
-        c.wait_recv()
+    arrive(lxy[1], lg.at[y])
     labs += lab_half(1)
     lcols.append(jnp.concatenate(labs[2:], axis=1))
     lcol = jnp.concatenate(labs, axis=1)
@@ -208,17 +206,23 @@
     for q in range(4):
         lcolb[q * 128 : (q + 1) * 128] = jnp.broadcast_to(labs[q].astype(F32), (128, 128)).T
 
-    def send_py(k):
-        return go(psend.at[1, xk[k]], precv_y.at[xk[k]], ypeer)
-
-    px = []
-
-    def take_py(k):
-        py[k].wait_recv()
-        v = psend[0, xk[k]].astype(F32) + precv_y[xk[k]].astype(F32)
-        psum[xk[k]] = v.astype(BF16)
-        if k:
-            px.append(go(psum.at[xk[k]], precv_x.at[k - 1], pid(xk[k], y, z)))
+    py2, px13, px = group(), group(), group()
+
+    def take_y2():
+        arrive(py2, precv_y)
+        v = psend[0, xk[2]].astype(F32) + precv_y[...].astype(F32)
+        psum[0] = v.astype(BF16)
+        go(psum.at[0], precv_x.at[0], pid(xk[2], y, z), px)
+
+    def take_x13():
+        arrive(px13, precv_x13)
+        v = [
+            psend[h, x].astype(F32) + precv_x13[0, h].astype(F32) + precv_x13[1, h].astype(F32)
+            for h in range(2)
+        ]
+        psum[1] = v[1].astype(BF16)
+        go(psum.at[1], precv_x.at[1], ypeer, px)
+        psum[2] = v[0].astype(BF16)
 
     def pick_labels():
         acc = jnp.zeros((B, D), F32)
@@ -234,10 +238,13 @@
             acc = acc + jnp.dot(
                 hot, hat[i * CB : (i + 1) * CB], preferred_element_type=F32
             )
+            turn_block(i)
         psend[...] = acc.astype(BF16).reshape(2, NX, 64, D)
 
     apart(pick_labels)
-    py = {k: send_py(k) for k in (2, 1, 3)}
+    go(psend.at[1, xk[2]], precv_y, ypeer, py2)
+    for i, k in enumerate((1, 3)):
+        go(psend.at[:, xk[k]], precv_x13.at[i], pid(xk[k], y, z), px13)
 
     def emb_half(h):
         e = xg[ys[h]].astype(F32)
@@ -273,19 +280,9 @@
         if h == 0:
             nown[...] = t
 
-    def n_send(hh):
-        return [
-            go(nsend.at[h, xk[k]], nrecv.at[i], xypeers[i])
-            for i, (k, h) in enumerate(XY)
-            if h == hh
-        ]
-
     emb_half(0)
     apart(lambda: cos_chunk(0))
-    for j in range(NZ):
-        yf[2, j].wait_recv()
-        xg2[1, j].wait_recv()
-        xg2[3, j].wait_recv()
+    arrive(rest, xg.at[ys[1], pl.ds(0, 3)])
     emb_half(1)
     apart(lambda: cos_chunk(1))
     t_part = jnp.sum(tacc[...], axis=0, keepdims=True)
@@ -307,47 +304,48 @@
     where_t = [ys[0] * 2, ys[0] * 2 + 1, ys[1] * 2, ys[1] * 2 + 1]
     for q in range(4):
         csend[0, pl.ds(where_t[q], 1)] = t_part[:, q * 128 : (q + 1) * 128]
-    cxy = [go(csend.at[0], crecv_xy.at[i], p) for i, p in enumerate(xypeers)]
-    py[0] = send_py(0)
-    take_py(2)
+    cxy = group()
+    for i, p in enumerate(xypeers):
+        go(csend.at[0], crecv_xy.at[i], p, cxy)
+    take_y2()
     apart(lambda: n_chunk(1))
-    nx = n_send(1)
-    take_py(1)
+    take_x13()
+    na, nx = group(), group()
+    for i, k in enumerate((1, 3)):
+        go(nsend.at[1, xk[k]], nrecv_a.at[i], pid(xk[k], y, z), na)
+    go(nsend.at[1, xk[2]], nrecv.at[0], pid(xk[2], ys[1], z), nx)
     apart(lambda: n_chunk(0))
-    nx += n_send(0)
-    take_py(3)
-    for c in cxy:
-        c.wait_recv()
+    for k in (1, 3, 2):
+        go(nsend.at[0, xk[k]], nrecv.at[k], pid(xk[k], y, z), nx)
+    arrive(cxy, crecv_xy)
     tot = csend[0]
     for i in range(7):
         tot = tot + crecv_xy[i]
     csend[1] = tot
-    cz = [go(csend.at[1], crecv_z.at[i], p) for i, p in enumerate(zpeers)]
-    take_py(0)
-    for c in px:
-        c.wait_recv()
-    s = psum[x].astype(F32)
-    for i in range(3):
-        s = s + precv_x[i].astype(F32)
+    cz = group()
+    for i, p in enumerate(zpeers):
+        go(csend.at[1], crecv_z.at[i], p, cz)
+    arrive(na, nrecv_a)
+    v = nsend[1, x].astype(F32) + nrecv_a[0].astype(F32) + nrecv_a[1].astype(F32)
+    nmid[...] = v.astype(BF16)
+    go(nmid, nrecv.at[4], ypeer, nx)
+    arrive(px, precv_x)
+    s = psum[2].astype(F32) + precv_x[0].astype(F32) + precv_x[1].astype(F32)
     pz[...] = s.astype(BF16).reshape(NZ, ROWS, D)
-    pzc = [
-        go(pz.at[(z + k) % NZ], precv_z.at[i], p)
-        for i, (k, p) in enumerate(zip(ZOFF[1:], zpeers))
-    ]
-    for c in nx:
-        c.wait_recv()
+    pzc = group()
+    for i, (k, p) in enumerate(zip(ZOFF[1:], zpeers)):
+        go(pz.at[(z + k) % NZ], precv_z.at[i], p, pzc)
+    arrive(nx, nrecv)
     s = nown[x]
-    for i in range(7):
+    for i in range(5):
         s = s + nrecv[i].astype(F32)
     s = s.reshape(NZ, ROWS, D)
     nz[...] = s
     nz_b[...] = s.astype(BF16)
-    nzc = [
-        go(nz_b.at[(z + k) % NZ], nrecv_z.at[i], p)
-        for i, (k, p) in enumerate(zip(ZOFF[1:], zpeers))
-    ]
-    for c in cz:
-        c.wait_recv()
+    nzc = group()
+    for i, (k, p) in enumerate(zip(ZOFF[1:], zpeers)):
+        go(nz_b.at[(z + k) % NZ], nrecv_z.at[i], p, nzc)
+    arrive(cz, crecv_z)
     tot = csend[1]
     for i in range(7):
         tot = tot + crecv_z[i]
@@ -373,8 +371,7 @@
 
     for i in range(NK):
         apart(functools.partial(class_block, i))
-    for c in pzc:
-        c.wait_recv()
+    arrive(pzc, precv_z)
     pick = pz[z].astype(F32)
     for i in range(7):
         pick = pick + precv_z[i].astype(F32)
@@ -393,15 +390,14 @@
     loss_ref[...] = jnp.sum(jnp.where(lan == sub, loss, 0.0), axis=0, keepdims=True)
     inv_t = 64.0 / tcol
     part = (sl * (jnp.exp2(LOG2E * sh) * inv_t - 64.0)) * pick
-    for c in nzc:
-        c.wait_recv()
+    arrive(nzc, nrecv_z)
     n = nz[z]
     for i in range(7):
         n = n + nrecv_z[i].astype(F32)
     g = n * inv_t + part
     grad_ref[...] = inv * (g - u * jnp.sum(u * g, axis=1, keepdims=True))
-    for c in pending:
-        c.wait_send()
+    for ref in sent:
+        pltpu.make_async_copy(ref, ref, send_sem.at[0]).wait()
 
 
 def write_kernel(
@@ -462,20 +458,23 @@
             pltpu.VMEM((7, 4, 128), F32),
             pltpu.VMEM((4, 128), F32),
             pltpu.VMEM((2, NX, 64, D), BF16),
-            pltpu.VMEM((NX, 64, D), BF16),
-            pltpu.VMEM((NX, 64, D), BF16),
+            pltpu.VMEM((64, D), BF16),
+            pltpu.VMEM((2, 2, 64, D), BF16),
             pltpu.VMEM((3, 64, D), BF16),
+            pltpu.VMEM((2, 64, D), BF16),
             pltpu.VMEM((NZ, ROWS, D), BF16),
             pltpu.VMEM((7, ROWS, D), BF16),
             pltpu.VMEM((2, NX, 64, D), BF16),
             pltpu.VMEM((NX, 64, D), F32),
-            pltpu.VMEM((7, 64, D), BF16),
+            pltpu.VMEM((2, 64, D), BF16),
+            pltpu.VMEM((64, D), BF16),
+            pltpu.VMEM((5, 64, D), BF16),
             pltpu.VMEM((NZ, ROWS, D), F32),
             pltpu.VMEM((NZ, ROWS, D), BF16),
             pltpu.VMEM((7, ROWS, D), BF16),
             pltpu.SemaphoreType.DMA((NCB + 2,)),
-            pltpu.SemaphoreType.DMA((130,)),
-            pltpu.SemaphoreType.DMA((130,)),
+            pltpu.SemaphoreType.DMA((1,)),
+            pltpu.SemaphoreType.DMA((38,)),
         ],
         compiler_params=pltpu.CompilerParams(
             collective_id=0, has_side_effects=True, vmem_limit_bytes=48 * 1024 * 1024

time: 46.3 us -> 44.2 us (0.955)
  Pallas kernels: 45.4 us -> 43.4 us
    pallas_call x1, Pallas kernels: 42 us -> 39.8 us  [whole(): pl.pallas_call(head_kernel, out_shape=(pltpu.VMEM((NK * CB, D), F32), plt...]
where the time goes in v6:
time: 44.2 us
  Pallas kernels  43.4 us (98%)
  between operations  0.8 us (2%)
    pallas_call x1, Pallas kernels, whole(): pl.pallas_call(head_kernel, out_shape=(pltpu.VMEM((NK * CB, D), F32), plt...  39.8 us
    pallas_call x1, Pallas kernels, whole(): pl.pallas_call(write_kernel, out_shape=(jax.ShapeDtypeStruct((C, D), F32)...  3.54 us

profile of v6, /device:TPU:8, one launch (start us, length us, event | category | flops | bytes accessed | tf_op | source)
XLA Modules:
  0.0 44.2 jit_solution(13463516146907418325)
XLA Ops:
  0.6 39.8 %head.1 = (f32[3072,512]{1,0:T(8,128)S(1)}, f32[8,512]{1,0:T(8,128)S(1)}, f32[1,128]{1,0:T(1,128)S(1)}, bf16[4096,512]{1,0:T(8,128)(2,1)S(1)}, bf16[4096,512]{1,...) custom-call(s32[8]{0:T(128)} %lab_hbm.1, bf16[8,512]{1,0:T(8,128)(2,1)} %emb_hbm.1, ...), custom_call_target="tpu_custom_call" | custom-call | tf_op jit(solution)/shard_map/head/pallas_call | solution.py:431
  40.5 3.5 %write.1 = (f32[4096,512]{1,0:T(8,128)}, f32[8,512]{1,0:T(8,128)}, f32[1,8]{1,0:T(1,128)}) custom-call(f32[3072,512]{1,0:T(8,128)S(1)} %get-tuple-element.14.val_ref, f32[8,512]{1,0:T(8,128)S(1)} %get-tuple-element.15.grad_ref, f32[1,128]{1,0:T(1,128)S(1)} %get-tuple-element.16.loss_ref, bf16[4096,512]{1,0:T(8,128)(2,1)S(1)} %get-tuple-element.17.wt_ref, ...), custom_call_target="tpu_custom_call" | custom-call | tf_op jit(solution)/shard_map/write/pallas_call | solution.py:484

commit v7 on v6

--- a/solution.py
+++ b/solution.py
@@ -23,7 +23,8 @@
 ZOFF = (0, 1, 7, 2, 6, 3, 5, 4)
 XY = ((1, 0), (3, 0), (2, 0), (0, 1), (1, 1), (3, 1), (2, 1))
 HB = B // 2
-NK = 6
+NK = 5
+HALVES = (slice(0, D // 2), slice(D // 2, D))
 LOG2E = 64.0 / math.log(2.0)
 
 
@@ -309,11 +310,13 @@
         go(csend.at[0], crecv_xy.at[i], p, cxy)
     take_y2()
     apart(lambda: n_chunk(1))
+    na, nx = (group(), group()), group()
+    for h, lanes in enumerate(HALVES):
+        for i, k in enumerate((1, 3)):
+            src = nsend.at[1, xk[k], :, lanes]
+            go(src, nrecv_a.at[i, :, lanes], pid(xk[k], y, z), na[h])
+    go(nsend.at[1, xk[2]], nrecv.at[0], pid(xk[2], ys[1], z), nx)
     take_x13()
-    na, nx = group(), group()
-    for i, k in enumerate((1, 3)):
-        go(nsend.at[1, xk[k]], nrecv_a.at[i], pid(xk[k], y, z), na)
-    go(nsend.at[1, xk[2]], nrecv.at[0], pid(xk[2], ys[1], z), nx)
     apart(lambda: n_chunk(0))
     for k in (1, 3, 2):
         go(nsend.at[0, xk[k]], nrecv.at[k], pid(xk[k], y, z), nx)
@@ -325,10 +328,12 @@
     cz = group()
     for i, p in enumerate(zpeers):
         go(csend.at[1], crecv_z.at[i], p, cz)
-    arrive(na, nrecv_a)
-    v = nsend[1, x].astype(F32) + nrecv_a[0].astype(F32) + nrecv_a[1].astype(F32)
-    nmid[...] = v.astype(BF16)
-    go(nmid, nrecv.at[4], ypeer, nx)
+    for h, lanes in enumerate(HALVES):
+        arrive(na[h], nrecv_a.at[:, :, lanes])
+        v = nsend[1, x, :, lanes].astype(F32)
+        v = v + nrecv_a[0, :, lanes].astype(F32) + nrecv_a[1, :, lanes].astype(F32)
+        nmid[:, lanes] = v.astype(BF16)
+        go(nmid.at[:, lanes], nrecv.at[4, :, lanes], ypeer, nx)
     arrive(px, precv_x)
     s = psum[2].astype(F32) + precv_x[0].astype(F32) + precv_x[1].astype(F32)
     pz[...] = s.astype(BF16).reshape(NZ, ROWS, D)

time: 44.2 us -> 43.3 us (0.980); the launches traced: 44.2 us -> 42.7 us
  Pallas kernels: 43.4 us -> 41.9 us
    pallas_call x1, Pallas kernels: 39.8 us -> 38.5 us  [whole(): pl.pallas_call(head_kernel, out_shape=(pltpu.VMEM((NK * CB, D), F32), plt...]
where the time goes in v7:
time: 43.3 us; the launch traced here: 42.7 us
  Pallas kernels  41.9 us (97%)
  between operations  0.8 us (2%)
    pallas_call x1, Pallas kernels, whole(): pl.pallas_call(head_kernel, out_shape=(pltpu.VMEM((NK * CB, D), F32), plt...  38.5 us
    pallas_call x1, Pallas kernels, whole(): pl.pallas_call(write_kernel, out_shape=(jax.ShapeDtypeStruct((C, D), F32)...  3.41 us

profile of v7, /device:TPU:8, one launch (start us, length us, event | category | flops | bytes accessed | tf_op | source)
XLA Modules:
  0.0 42.7 jit_solution(458545183865807446)
XLA Ops:
  0.6 38.5 %head.1 = (f32[2560,512]{1,0:T(8,128)S(1)}, f32[8,512]{1,0:T(8,128)S(1)}, f32[1,128]{1,0:T(1,128)S(1)}, bf16[4096,512]{1,0:T(8,128)(2,1)S(1)}, bf16[4096,512]{1,...) custom-call(s32[8]{0:T(128)} %lab_hbm.1, bf16[8,512]{1,0:T(8,128)(2,1)} %emb_hbm.1, ...), custom_call_target="tpu_custom_call" | custom-call | tf_op jit(solution)/shard_map/head/pallas_call | solution.py:436
  39.2 3.4 %write.1 = (f32[4096,512]{1,0:T(8,128)}, f32[8,512]{1,0:T(8,128)}, f32[1,8]{1,0:T(1,128)}) custom-call(f32[2560,512]{1,0:T(8,128)S(1)} %get-tuple-element.14.val_ref, f32[8,512]{1,0:T(8,128)S(1)} %get-tuple-element.15.grad_ref, f32[1,128]{1,0:T(1,128)S(1)} %get-tuple-element.16.loss_ref, bf16[4096,512]{1,0:T(8,128)(2,1)S(1)} %get-tuple-element.17.wt_ref, ...), custom_call_target="tpu_custom_call" | custom-call | tf_op jit(solution)/shard_map/write/pallas_call | solution.py:489

commit v8 on v7

--- a/solution.py
+++ b/solution.py
@@ -67,18 +67,14 @@
     for p in zpeers + xypeers:
         pl.semaphore_signal(barrier, inc=1, device_id={"cls": p})
 
-    def cen_copy(i):
-        rows = pl.ds(i * CB, CB)
-        return pltpu.make_async_copy(cen_ref.at[rows], raw_ref.at[rows], cen_sem.at[i])
-
+    whole_cen = pltpu.make_async_copy(cen_ref, raw_ref, cen_sem.at[0])
     small = [
-        pltpu.make_async_copy(lab_hbm, lab_ref, cen_sem.at[NCB]),
-        pltpu.make_async_copy(emb_hbm, emb_ref, cen_sem.at[NCB + 1]),
+        pltpu.make_async_copy(lab_hbm, lab_ref, cen_sem.at[1]),
+        pltpu.make_async_copy(emb_hbm, emb_ref, cen_sem.at[2]),
     ]
     for c in small:
         c.start()
-    for i in range(NCB):
-        cen_copy(i).start()
+    whole_cen.start()
 
     lane = lax.broadcasted_iota(jnp.int32, (1, 128), 1)
     off = (x % 2) * 64 + z * ROWS
@@ -91,7 +87,6 @@
     xg[y, x, z] = emb_ref[...]
 
     def norm_block(i):
-        cen_copy(i).wait()
         rows = pl.ds(i * CB, CB)
         v = raw_ref[rows].astype(F32)
         inv = lax.rsqrt(jnp.sum(v * v, axis=1, keepdims=True) + EPS)
@@ -128,7 +123,7 @@
     for p in zpeers:
         go(lsl, lsl, p, lz)
     ez = [group() for p in zpeers]
-    for g, p in zip(ez, zpeers):
+    for g, p in reversed(list(zip(ez, zpeers))):
         go(emb_ref, xg.at[y, x, z], p, g)
     xf = [group() for j in range(NZ)]
     yf = [group() for j in range(NZ)]
@@ -170,6 +165,7 @@
         arrive(xf[j], xg.at[y, x, pl.ds(0, 3)])
         forward_y(2, j)
 
+    whole_cen.wait()
     do(NCB)
     on_z(1)
     on_z(2)
@@ -318,7 +314,7 @@
     go(nsend.at[1, xk[2]], nrecv.at[0], pid(xk[2], ys[1], z), nx)
     take_x13()
     apart(lambda: n_chunk(0))
-    for k in (1, 3, 2):
+    for k in (2, 1, 3):
         go(nsend.at[0, xk[k]], nrecv.at[k], pid(xk[k], y, z), nx)
     arrive(cxy, crecv_xy)
     tot = csend[0]
@@ -326,7 +322,7 @@
         tot = tot + crecv_xy[i]
     csend[1] = tot
     cz = group()
-    for i, p in enumerate(zpeers):
+    for i, p in reversed(list(enumerate(zpeers))):
         go(csend.at[1], crecv_z.at[i], p, cz)
     for h, lanes in enumerate(HALVES):
         arrive(na[h], nrecv_a.at[:, :, lanes])
@@ -338,7 +334,7 @@
     s = psum[2].astype(F32) + precv_x[0].astype(F32) + precv_x[1].astype(F32)
     pz[...] = s.astype(BF16).reshape(NZ, ROWS, D)
     pzc = group()
-    for i, (k, p) in enumerate(zip(ZOFF[1:], zpeers)):
+    for i, (k, p) in reversed(list(enumerate(zip(ZOFF[1:], zpeers)))):
         go(pz.at[(z + k) % NZ], precv_z.at[i], p, pzc)
     arrive(nx, nrecv)
     s = nown[x]
@@ -348,7 +344,7 @@
     nz[...] = s
     nz_b[...] = s.astype(BF16)
     nzc = group()
-    for i, (k, p) in enumerate(zip(ZOFF[1:], zpeers)):
+    for i, (k, p) in reversed(list(enumerate(zip(ZOFF[1:], zpeers)))):
         go(nz_b.at[(z + k) % NZ], nrecv_z.at[i], p, nzc)
     arrive(cz, crecv_z)
     tot = csend[1]
@@ -477,7 +473,7 @@
             pltpu.VMEM((NZ, ROWS, D), F32),
             pltpu.VMEM((NZ, ROWS, D), BF16),
             pltpu.VMEM((7, ROWS, D), BF16),
-            pltpu.SemaphoreType.DMA((NCB + 2,)),
+            pltpu.SemaphoreType.DMA((3,)),
             pltpu.SemaphoreType.DMA((1,)),
             pltpu.SemaphoreType.DMA((38,)),
         ],

time: 43.3 us -> 42.5 us (0.982)
  Pallas kernels: 41.9 us -> 41.3 us
    pallas_call x1, Pallas kernels: 38.5 us -> 37.9 us  [whole(): pl.pallas_call(head_kernel, out_shape=(pltpu.VMEM((NK * CB, D), F32), plt...]
where the time goes in v8:
time: 42.5 us; the launch traced here: 42.1 us
  Pallas kernels  41.3 us (97%)
  between operations  0.8 us (2%)
    pallas_call x1, Pallas kernels, whole(): pl.pallas_call(head_kernel, out_shape=(pltpu.VMEM((NK * CB, D), F32), plt...  37.9 us
    pallas_call x1, Pallas kernels, whole(): pl.pallas_call(write_kernel, out_shape=(jax.ShapeDtypeStruct((C, D), F32)...  3.41 us

profile of v8, /device:TPU:8, one launch (start us, length us, event | category | flops | bytes accessed | tf_op | source)
XLA Modules:
  0.0 42.1 jit_solution(13698710468228020052)
XLA Ops:
  0.6 37.9 %head.1 = (f32[2560,512]{1,0:T(8,128)S(1)}, f32[8,512]{1,0:T(8,128)S(1)}, f32[1,128]{1,0:T(1,128)S(1)}, bf16[4096,512]{1,0:T(8,128)(2,1)S(1)}, bf16[4096,512]{1,...) custom-call(s32[8]{0:T(128)} %lab_hbm.1, bf16[8,512]{1,0:T(8,128)(2,1)} %emb_hbm.1, ...), custom_call_target="tpu_custom_call" | custom-call | tf_op jit(solution)/shard_map/head/pallas_call | solution.py:432
  38.5 3.4 %write.1 = (f32[4096,512]{1,0:T(8,128)}, f32[8,512]{1,0:T(8,128)}, f32[1,8]{1,0:T(1,128)}) custom-call(f32[2560,512]{1,0:T(8,128)S(1)} %get-tuple-element.14.val_ref, f32[8,512]{1,0:T(8,128)S(1)} %get-tuple-element.15.grad_ref, f32[1,128]{1,0:T(1,128)S(1)} %get-tuple-element.16.loss_ref, bf16[4096,512]{1,0:T(8,128)(2,1)S(1)} %get-tuple-element.17.wt_ref, ...), custom_call_target="tpu_custom_call" | custom-call | tf_op jit(solution)/shard_map/write/pallas_call | solution.py:485

commit v9 on v8

--- a/solution.py
+++ b/solution.py
@@ -24,7 +24,7 @@
 XY = ((1, 0), (3, 0), (2, 0), (0, 1), (1, 1), (3, 1), (2, 1))
 HB = B // 2
 NK = 5
-HALVES = (slice(0, D // 2), slice(D // 2, D))
+HALVES = tuple(slice(i * 128, (i + 1) * 128) for i in range(4))
 LOG2E = 64.0 / math.log(2.0)
 
 
@@ -306,7 +306,7 @@
         go(csend.at[0], crecv_xy.at[i], p, cxy)
     take_y2()
     apart(lambda: n_chunk(1))
-    na, nx = (group(), group()), group()
+    na, nx = [group() for _ in HALVES], group()
     for h, lanes in enumerate(HALVES):
         for i, k in enumerate((1, 3)):
             src = nsend.at[1, xk[k], :, lanes]
@@ -475,7 +475,7 @@
             pltpu.VMEM((7, ROWS, D), BF16),
             pltpu.SemaphoreType.DMA((3,)),
             pltpu.SemaphoreType.DMA((1,)),
-            pltpu.SemaphoreType.DMA((38,)),
+            pltpu.SemaphoreType.DMA((40,)),
         ],
         compiler_params=pltpu.CompilerParams(
             collective_id=0, has_side_effects=True, vmem_limit_bytes=48 * 1024 * 1024

time: 42.5 us -> 42.4 us (level)
  no operation moved by 1% of the time
where the time goes in v9:
time: 42.4 us; the launch traced here: 42 us
  Pallas kernels  41.2 us (97%)
  between operations  0.8 us (2%)
    pallas_call x1, Pallas kernels, whole(): pl.pallas_call(head_kernel, out_shape=(pltpu.VMEM((NK * CB, D), F32), plt...  37.8 us
    pallas_call x1, Pallas kernels, whole(): pl.pallas_call(write_kernel, out_shape=(jax.ShapeDtypeStruct((C, D), F32)...  3.41 us

profile of v9, /device:TPU:8, one launch (start us, length us, event | category | flops | bytes accessed | tf_op | source)
XLA Modules:
  0.0 42.0 jit_solution(922101975852639839)
XLA Ops:
  0.6 37.8 %head.1 = (f32[2560,512]{1,0:T(8,128)S(1)}, f32[8,512]{1,0:T(8,128)S(1)}, f32[1,128]{1,0:T(1,128)S(1)}, bf16[4096,512]{1,0:T(8,128)(2,1)S(1)}, bf16[4096,512]{1,...) custom-call(s32[8]{0:T(128)} %lab_hbm.1, bf16[8,512]{1,0:T(8,128)(2,1)} %emb_hbm.1, ...), custom_call_target="tpu_custom_call" | custom-call | tf_op jit(solution)/shard_map/head/pallas_call | solution.py:432
  38.4 3.4 %write.1 = (f32[4096,512]{1,0:T(8,128)}, f32[8,512]{1,0:T(8,128)}, f32[1,8]{1,0:T(1,128)}) custom-call(f32[2560,512]{1,0:T(8,128)S(1)} %get-tuple-element.14.val_ref, f32[8,512]{1,0:T(8,128)S(1)} %get-tuple-element.15.grad_ref, f32[1,128]{1,0:T(1,128)S(1)} %get-tuple-element.16.loss_ref, bf16[4096,512]{1,0:T(8,128)(2,1)S(1)} %get-tuple-element.17.wt_ref, ...), custom_call_target="tpu_custom_call" | custom-call | tf_op jit(solution)/shard_map/write/pallas_call | solution.py:485
